TPU v7x, 32 devices: a whole 2x2x4 slice. The times are simulated.
32 devices in a mesh: rep: 4 (over x, y), dp: 8 (over z, core).
Axes of the slice: x: 2, y: 2, z: 4, core: 2. Of those that a mesh axis runs over, the one named last changes fastest.
Arguments:
- x: bfloat16 [32, 2048, 768], P(('rep', 'dp')), parts along dimension 0
- dy: bfloat16 [32, 2048, 768], P(('rep', 'dp')), parts along dimension 0
- w_gate: bfloat16 [2, 768, 1792], replicated
- w_up: bfloat16 [2, 768, 1792], replicated
- w_down: bfloat16 [2, 1792, 768], replicated
- m_w_gate: float32 [2, 768, 1792], P(None, 'dp')
- m_w_up: float32 [2, 768, 1792], P(None, 'dp')
- m_w_down: float32 [2, 1792, 768], P(None, 'dp')
- v_w_gate: float32 [2, 768, 1792], P(None, 'dp')
- v_w_up: float32 [2, 768, 1792], P(None, 'dp')
- v_w_down: float32 [2, 1792, 768], P(None, 'dp')
Outputs:
- output 1: bfloat16 [8, 768, 1792], P('rep'), parts along dimension 0
- output 2: bfloat16 [8, 768, 1792], P('rep'), parts along dimension 0
- output 3: bfloat16 [8, 1792, 768], P('rep'), parts along dimension 0
- output 4: float32 [8, 768, 1792], P('rep', 'dp'), parts along dimension 0
- output 5: float32 [8, 768, 1792], P('rep', 'dp'), parts along dimension 0
- output 6: float32 [8, 1792, 768], P('rep', 'dp'), parts along dimension 0
- output 7: float32 [8, 768, 1792], P('rep', 'dp'), parts along dimension 0
- output 8: float32 [8, 768, 1792], P('rep', 'dp'), parts along dimension 0
- output 9: float32 [8, 1792, 768], P('rep', 'dp'), parts along dimension 0
There are 4 independent parts. A program takes and returns all parts, laid end to end along the dimension named above; an argument that names none is the same for every part.
All inputs are finite; a program needn't handle non-finite values.
Results may differ from a plain program's by a relative error of at most 0.022.
Values are sent between devices in bfloat16 or wider.
A program may use at most 2 GiB of HBM per device.

v0:
```python
import jax
import jax.numpy as jnp
from jax import lax

NAMES = ("w_gate", "w_up", "w_down")


def matmul(a, w):
    return jnp.dot(a, w, preferred_element_type=jnp.float32).astype(jnp.bfloat16)


def normed(h):
    wide = h.astype(jnp.float32)
    scale = lax.rsqrt(jnp.mean(wide**2, -1, keepdims=True) + 1e-6)
    return (wide * scale).astype(jnp.bfloat16)


def layer(h, w):
    a = normed(h)
    gate = jnp.dot(a, w["w_gate"], preferred_element_type=jnp.float32)
    up = jnp.dot(a, w["w_up"], preferred_element_type=jnp.float32)
    return h + matmul((jax.nn.silu(gate) * up).astype(jnp.bfloat16), w["w_down"])


def adamw(w, m, v, g):
    m = 0.9 * m + 0.1 * g
    v = 0.95 * v + 0.05 * g * g
    step = m * lax.rsqrt(v + 1e-8) + 0.1 * w
    return (w - 0.02 * step).astype(jnp.bfloat16), m, v


def clipped(gradients, sum_of_squares, count):
    factor = jnp.minimum(1.0, 0.5 * lax.rsqrt(sum_of_squares / count + 1e-30))
    return [g * factor for g in gradients]


def stack(weights, h):
    for number in range(weights["w_gate"].shape[0]):
        h = layer(h, {name: w[number] for name, w in weights.items()})
    return h


def solution(mesh):
    groups = mesh.shape["rep"]

    def step(x, dy, *arrays):
        weights, m, v = (arrays[i : i + 3] for i in (0, 3, 6))
        x, dy = (t.reshape(groups, -1, *t.shape[1:]) for t in (x, dy))

        def of_a_group(x, dy):
            _, back = jax.vjp(lambda w: stack(w, x), dict(zip(NAMES, weights, strict=True)))
            by_weights = back(dy)[0]
            gradients = [by_weights[name].astype(jnp.float32) for name in NAMES]
            gradients = clipped(gradients, sum(jnp.sum(g * g) for g in gradients), sum(g.size for g in gradients))
            new = [adamw(w.astype(jnp.float32), m, v, g) for w, m, v, g in zip(weights, m, v, gradients, strict=True)]
            return tuple(one[which] for which in range(3) for one in new)

        return tuple(t.reshape(-1, *t.shape[2:]) for t in jax.vmap(of_a_group)(x, dy))

    return step
```

profile of v0, /device:TPU:0, one launch (start us, length us, event | category | flops | bytes accessed | tf_op | source)
XLA Modules:
  0.0 740.1 jit_solution(15624715579582388627)
XLA Ops:
  7.2 2.7 fusion.35
  10.0 4.6 copy
  14.6 7.8 %fusion.77 = f32[2048,1792]{1,0:T(8,128)S(1)} fusion(bf16[2,768,1792]{2,1,0:T(8,128)(2,1)} %param, bf16[1,2048,768]{2,1,0:T(8,128)(2,1)S(1)} %copy-done.2, f32[2048]{0:T(1024)S(1)} %add_rsqrt_fusion), kind=kOutput, calls=%fused_computation.88 | convolution fusion | flops 5641863168 | bytes 20586496 | tf_op jit(solution)/vmap(jvp())/dot_general | solution.py:20
  22.5 13.2 %fusion.75 = f32[2048,1792]{1,0:T(8,128)S(1)} fusion(bf16[2,768,1792]{2,1,0:T(8,128)(2,1)} %param.3, bf16[1,2048,768]{2,1,0:T(8,128)(2,1)} %param.2, f32[2048]{0:T(1024)S(1)} %add_rsqrt_fusion), kind=kOutput, calls=%fused_computation.86 | convolution fusion | flops 5641863168 | bytes 20586496 | tf_op jit(solution)/vmap(jvp())/dot_general | solution.py:21
  35.7 7.4 %fusion.26 = bf16[2048,1792]{1,0:T(8,128)(2,1)} fusion(f32[2048,1792]{1,0:T(8,128)S(1)} %fusion.75, f32[2048,1792]{1,0:T(8,128)S(1)} %fusion.77), kind=kLoop, calls=%fused_computation.44 | loop fusion | flops 22020096 | bytes 36700160
  43.1 10.1 %fusion.39 = (f32[2048]{0:T(1024)S(1)}, bf16[1,1,2048,768]{2,3,1,0:T(8,128)(2,1)S(1)}) fusion(bf16[2048,1792]{1,0:T(8,128)(2,1)} %fusion.26, bf16[2,1792,768]{2,1,0:T(8,128)(2,1)} %param.4, bf16[1,2048,768]{1,2,0:T(8,128)(2,1)} %copy), kind=kOutput, calls=%fused_computation.56 | convolution fusion | flops 5645006848 | bytes 16392192 | tf_op jit(solution)/vmap(jvp())/dot_general | solution.py:9
  53.2 12.1 %fusion.66 = f32[2048,1792]{1,0:T(8,128)} fusion(bf16[2,768,1792]{2,1,0:T(8,128)(2,1)} %param, bf16[1,1,2048,768]{2,3,1,0:T(8,128)(2,1)S(1)} %get-tuple-element.10, f32[2048]{0:T(1024)S(1)} %bitcast.357), kind=kOutput, calls=%fused_computation.77 | convolution fusion | flops 5641863168 | bytes 20586496 | tf_op jit(solution)/vmap(jvp())/dot_general | solution.py:20
  65.4 11.0 %fusion.69 = f32[2048,1792]{1,0:T(8,128)} fusion(bf16[2,768,1792]{2,1,0:T(8,128)(2,1)} %param.3, bf16[1,1,2048,768]{2,3,1,0:T(8,128)(2,1)S(1)} %get-tuple-element.10, f32[2048]{0:T(1024)S(1)} %bitcast.358), kind=kOutput, calls=%fused_computation.80 | convolution fusion | flops 5641863168 | bytes 20586496 | tf_op jit(solution)/vmap(jvp())/dot_general | solution.py:21
  76.4 8.5 %convolution_convert_fusion.1 = bf16[2048,1792]{1,0:T(8,128)(2,1)} fusion(bf16[1,2048,768]{2,1,0:T(8,128)(2,1)S(1)} %copy-done.5, bf16[2,1792,768]{2,1,0:T(8,128)(2,1)S(1)} %bitcast.353), kind=kOutput, calls=%fused_computation.43 | convolution fusion | flops 5640814592 | bytes 13238272 | tf_op jit(solution)/vmap(transpose(jvp()))/dot_general | solution.py:9
  84.9 3.2 copy.1
  88.1 13.4 %fusion.6 = bf16[2048,1792]{1,0:T(8,128)(2,1)S(1)} fusion(f32[2048,1792]{1,0:T(8,128)} %fusion.66, f32[2048,1792]{1,0:T(8,128)} %fusion.69, bf16[2048,1792]{1,0:T(8,128)(2,1)} %convolution_convert_fusion.1), kind=kLoop, calls=%fused_computation.11 | loop fusion | flops 44040192 | bytes 44040192
  101.6 2.9 copy-done.3
  104.5 7.6 %convolution_convert_fusion.2 = bf16[2048,768]{0,1:T(8,128)(2,1)S(1)} fusion(bf16[2048,1792]{1,0:T(8,128)(2,1)S(1)} %fusion.6, bf16[2,768,1792]{2,1,0:T(8,128)(2,1)} %param), kind=kOutput, calls=%fused_computation.66 | convolution fusion | flops 5637144576 | bytes 13238272 | tf_op jit(solution)/vmap(transpose(jvp()))/dot_general | solution.py:20
  112.1 13.0 %fusion.41 = (f32[2048]{0:T(1024)S(1)}, bf16[2048,768]{0,1:T(8,128)(2,1)}) fusion(bf16[1,1,2048,768]{2,3,1,0:T(8,128)(2,1)S(1)} %copy-done.9, bf16[2048,768]{0,1:T(8,128)(2,1)S(1)} %convolution_convert_fusion.2, bf16[2,768,1792]{2,1,0:T(8,128)(2,1)} %param.3, bf16[2048,1792]{1,0:T(8,128)(2,1)} %convolution_convert_fusion.1, f32[2048,1792]{1,0:T(8,128)} %fusion.66), kind=kOutput, calls=%fused_computation.58 | convolution fusion | flops 5668599808 | bytes 34217984 | tf_op jit(solution)/vmap(transpose(jvp()))/dot_general | solution.py:21
  125.2 4.1 fusion.60
  129.3 1.7 copy-done.11
  131.0 10.0 %convolution_bitcast_fusion = f32[1,1792,768]{2,1,0:T(8,128)} fusion(bf16[2048,1792]{1,0:T(8,128)(2,1)} %fusion.26, bf16[2048,768]{0,1:T(8,128)(2,1)S(1)} %fusion.60), kind=kOutput, calls=%fused_computation.63 | convolution fusion | flops 5637144576 | bytes 15990784 | tf_op jit(solution)/vmap(transpose(jvp()))/dot_general | solution.py:9
  141.0 1.8 copy-done.6
  142.8 14.4 %fusion.42 = f32[1,1792,768]{2,1,0:T(8,128)} fusion(f32[2048,1792]{1,0:T(8,128)} %fusion.69, f32[2048,1792]{1,0:T(8,128)} %fusion.66, bf16[1,2048,768]{2,1,0:T(8,128)(2,1)S(1)} %copy-done.6), kind=kOutput, calls=%fused_computation.60 | convolution fusion | flops 5659164672 | bytes 38010880 | tf_op jit(solution)/vmap(transpose(jvp()))/dot_general | solution.py:9
  157.3 8.8 %convolution_convert_fusion = bf16[2048,1792]{1,0:T(8,128)(2,1)S(1)} fusion(bf16[2048,768]{0,1:T(8,128)(2,1)} %copy-done.11, bf16[2,1792,768]{2,1,0:T(8,128)(2,1)} %param.4), kind=kOutput, calls=%fused_computation.42 | convolution fusion | flops 5640814592 | bytes 13238272 | tf_op jit(solution)/vmap(transpose(jvp()))/dot_general | solution.py:9
  166.1 3.0 copy-done.17
  169.1 11.9 %fusion.48 = f32[1,768,1792]{2,1,0:T(8,128)} fusion(bf16[2048,1792]{1,0:T(8,128)(2,1)S(1)} %convolution_convert_fusion, f32[2048,1792]{1,0:T(8,128)} %copy-done, bf16[1,2048,768]{1,2,0:T(8,128)(2,1)S(1)} %copy-done.7, f32[2048]{0:T(1024)S(1)} %copy-done.15), kind=kOutput, calls=%fused_computation.62 | convolution fusion | flops 5663883264 | bytes 30679040 | tf_op jit(solution)/vmap(transpose(jvp()))/dot_general | solution.py:21
  181.1 13.9 %fusion.45 = f32[1,768,1792]{2,1,0:T(8,128)} fusion(bf16[2048,1792]{1,0:T(8,128)(2,1)} %convolution_convert_fusion.1, f32[2048,1792]{1,0:T(8,128)} %fusion.66, bf16[1,1,2048,768]{2,3,1,0:T(8,128)(2,1)} %copy-done.8, f32[2048]{0:T(1024)S(1)} %bitcast.360), kind=kOutput, calls=%fused_computation.61 | convolution fusion | flops 5663883264 | bytes 30679040 | tf_op jit(solution)/vmap(transpose(jvp()))/dot_general | solution.py:21
  195.1 17.5 %fusion.51 = f32[1,768,1792]{2,1,0:T(8,128)} fusion(f32[2048,1792]{1,0:T(8,128)} %copy-done, f32[2048,1792]{1,0:T(8,128)} %copy-done.1, bf16[2048,1792]{1,0:T(8,128)(2,1)} %copy-done.17, bf16[1,2048,768]{1,2,0:T(8,128)(2,1)S(1)} %copy-done.7, f32[2048]{0:T(1024)S(1)} %copy-done.15), kind=kOutput, calls=%fused_computation.65 | convolution fusion | flops 5682233344 | bytes 45359104 | tf_op jit(solution)/vmap(transpose(jvp()))/dot_general | solution.py:20
  212.7 1.8 copy-done.10
  214.5 10.6 %convolution_bitcast_fusion.1 = f32[1,768,1792]{2,1,0:T(8,128)} fusion(bf16[2048,1792]{1,0:T(8,128)(2,1)} %copy-done.3, bf16[1,1,2048,768]{2,3,1,0:T(8,128)(2,1)S(1)} %copy-done.10, f32[2048]{0:T(1024)S(1)} %bitcast.361), kind=kOutput, calls=%fused_computation.64 | convolution fusion | flops 5641863168 | bytes 15998976 | tf_op jit(solution)/vmap(transpose(jvp()))/dot_general | solution.py:20
  227.1 1.1 convert_bitcast_fusion.3
  228.2 41.1 %reduce-scatter.27.cloned.1.call-done = f32[1,224,768]{2,1,0:T(8,128)} async-done(((f32[1,1792,768]{2,1,0:T(8,128)}), f32[1,224,768]{2,1,0:T(8,128)}) %reduce-scatter.27.cloned.1.call-update) | async-done | bytes 688144
  269.3 1.1 convert_bitcast_fusion.4
  271.4 61.8 %reduce-scatter.25.cloned.1.call-done = f32[1,96,1792]{2,1,0:T(8,128)} async-done(((f32[1,768,1792]{2,1,0:T(8,128)}), f32[1,96,1792]{2,1,0:T(8,128)}) %reduce-scatter.25.cloned.1.call-update) | async-done | bytes 688144
  333.2 1.1 convert_bitcast_fusion.5
  334.3 62.0 %reduce-scatter.23.cloned.1.call-done = f32[1,96,1792]{2,1,0:T(8,128)} async-done(((f32[1,768,1792]{2,1,0:T(8,128)}), f32[1,96,1792]{2,1,0:T(8,128)}) %reduce-scatter.23.cloned.1.call-update) | async-done | bytes 688144
  396.4 1.1 convert_bitcast_fusion.6
  398.4 61.6 %reduce-scatter.21.cloned.1.call-done = f32[1,96,1792]{2,1,0:T(8,128)} async-done(((f32[1,768,1792]{2,1,0:T(8,128)}), f32[1,96,1792]{2,1,0:T(8,128)}) %reduce-scatter.21.cloned.1.call-update) | async-done | bytes 688144
  460.1 1.1 convert_bitcast_fusion.7
  461.2 62.6 %reduce-scatter.19.cloned.1.call-done = f32[1,96,1792]{2,1,0:T(8,128)} async-done(((f32[1,768,1792]{2,1,0:T(8,128)}), f32[1,96,1792]{2,1,0:T(8,128)}) %reduce-scatter.19.cloned.1.call-update) | async-done | bytes 688144
  523.8 1.1 convert_bitcast_fusion.8
  527.8 15.0 %all-reduce.16 = f32[1]{0:T(128)} all-reduce(f32[1]{0:T(128)} %bitcast.50), channel_id=5, replica_groups=mesh['rep'=4,'dp'=8] {'dp'}, use_global_device_ids=true, to_apply=%region_3.4.clone | all-reduce | flops 1 | bytes 8 | tf_op jit(solution)/vmap()/reduce_sum | solution.py:54
  543.5 4.1 fusion.129
  547.6 4.6 fusion.130
  552.3 4.0 fusion.131
  556.4 47.2 %all-gather.14.cloned.1.call-done = bf16[1,2,1792,768]{3,2,1,0:T(8,128)(2,1)} async-done(((bf16[1,2,224,768]{3,2,1,0:T(8,128)(2,1)}), bf16[1,2,1792,768]{3,2,1,0:T(8,128)(2,1)}) %all-gather.14.cloned.1.call-update) | async-done | bytes 5505040 | tf_op jit(solution)/reshape | solution.py:58
  603.6 58.6 %all-gather.12.cloned.1.call-done = bf16[1,2,768,1792]{3,2,1,0:T(8,128)(2,1)} async-done(((bf16[1,2,96,1792]{3,2,1,0:T(8,128)(2,1)}), bf16[1,2,768,1792]{3,2,1,0:T(8,128)(2,1)}) %all-gather.12.cloned.1.call-update) | async-done | bytes 5505040 | tf_op jit(solution)/reshape | solution.py:58
  662.2 58.6 %all-gather.10.cloned.1.call-done = bf16[1,2,768,1792]{3,2,1,0:T(8,128)(2,1)} async-done(((bf16[1,2,96,1792]{3,2,1,0:T(8,128)(2,1)}), bf16[1,2,768,1792]{3,2,1,0:T(8,128)(2,1)}) %all-gather.10.cloned.1.call-update) | async-done | bytes 5505040 | tf_op jit(solution)/reshape | solution.py:58
  720.8 5.9 copy.5
  726.7 2.8 copy.6
  729.6 1.1 slice-done.1
  730.7 2.4 copy.7
  (67 shorter events, 4.8 us)
Async XLA Ops:
  7.2 7.4 %copy-start.2 = (bf16[1,2048,768]{2,1,0:T(8,128)(2,1)S(1)}, bf16[1,2048,768]{2,1,0:T(8,128)(2,1)}, u32[]{:S(2)}) copy-start(bf16[1,2048,768]{2,1,0:T(8,128)(2,1)} %param.2) | copy-start | bytes 9437188
  7.2 219.9 %reduce-scatter.29.cloned.1.call-start = ((), (), s32[]{:S(2)}) async-start(), calls=%async_computation.14 | async-start | bytes 6193152
  14.6 7.9 %copy-start.14 = (f32[2048]{0:T(1024)}, f32[2048]{0:T(1024)S(1)}, u32[]{:S(2)}) copy-start(f32[2048]{0:T(1024)S(1)} %add_rsqrt_fusion) | copy-start | bytes 24580
  22.5 13.2 %copy-start = (f32[2048,1792]{1,0:T(8,128)}, f32[2048,1792]{1,0:T(8,128)S(1)}, u32[]{:S(2)}) copy-start(f32[2048,1792]{1,0:T(8,128)S(1)} %fusion.77) | copy-start | bytes 44040196
  35.7 7.4 %copy-start.1 = (f32[2048,1792]{1,0:T(8,128)}, f32[2048,1792]{1,0:T(8,128)S(1)}, u32[]{:S(2)}) copy-start(f32[2048,1792]{1,0:T(8,128)S(1)} %fusion.75) | copy-start | bytes 44040196
  43.1 33.3 %slice-start.2 = ((s8[5505024]{0:T(1024)(128)(4,1)}), s8[4194304]{0:T(1024)(128)(4,1)S(1)}, s32[]{:S(2)}) async-start(s8[5505024]{0:T(1024)(128)(4,1)} %bitcast.352), calls=%async_computation.17 | async-start | bytes 8388608
  53.2 12.2 %copy-start.8 = (bf16[1,1,2048,768]{2,3,1,0:T(8,128)(2,1)}, bf16[1,1,2048,768]{2,3,1,0:T(8,128)(2,1)S(1)}, u32[]{:S(2)}) copy-start(bf16[1,1,2048,768]{2,3,1,0:T(8,128)(2,1)S(1)} %get-tuple-element.10) | copy-start | bytes 9437188
  53.2 23.2 %slice-start.3 = ((s8[5505024]{0:T(1024)(128)(4,1)}), s8[1310720]{0:T(1024)(128)(4,1)S(1)}, s32[]{:S(2)}) async-start(s8[5505024]{0:T(1024)(128)(4,1)} %bitcast.352), calls=%async_computation.18 | async-start | bytes 2621440
  65.4 11.0 %copy-start.5 = (bf16[1,2048,768]{2,1,0:T(8,128)(2,1)S(1)}, bf16[1,2048,768]{2,1,0:T(8,128)(2,1)}, u32[]{:S(2)}) copy-start(bf16[1,2048,768]{2,1,0:T(8,128)(2,1)} %param.5) | copy-start | bytes 9437188
  101.5 3.0 copy-start.3
  104.5 7.6 %copy-start.9 = (bf16[1,1,2048,768]{2,3,1,0:T(8,128)(2,1)S(1)}, bf16[1,1,2048,768]{2,3,1,0:T(8,128)(2,1)}, u32[]{:S(2)}) copy-start(bf16[1,1,2048,768]{2,3,1,0:T(8,128)(2,1)} %copy-done.8) | copy-start | bytes 9437188
  129.3 1.7 copy-start.11
  140.9 1.9 copy-start.6
  141.0 128.4 %reduce-scatter.27.cloned.1.call-start = ((), (), s32[]{:S(2)}) async-start(), calls=%async_computation.13 | async-start | bytes 6193152
  157.2 11.9 %copy-start.7 = (bf16[1,2048,768]{1,2,0:T(8,128)(2,1)S(1)}, bf16[1,2048,768]{1,2,0:T(8,128)(2,1)}, u32[]{:S(2)}) copy-start(bf16[1,2048,768]{1,2,0:T(8,128)(2,1)} %copy) | copy-start | bytes 9437188
  157.2 11.9 %copy-start.15 = (f32[2048]{0:T(1024)S(1)}, f32[2048]{0:T(1024)}, u32[]{:S(2)}) copy-start(f32[2048]{0:T(1024)} %copy-done.14) | copy-start | bytes 24580
  157.2 176.0 %reduce-scatter.25.cloned.1.call-start = ((), (), s32[]{:S(2)}) async-start(), calls=%async_computation.12 | async-start | bytes 6193152
  166.1 3.0 copy-start.17
  181.1 215.3 %reduce-scatter.23.cloned.1.call-start = ((), (), s32[]{:S(2)}) async-start(), calls=%async_computation.11 | async-start | bytes 6193152
  195.1 265.0 %reduce-scatter.21.cloned.1.call-start = ((), (), s32[]{:S(2)}) async-start(), calls=%async_computation.10 | async-start | bytes 6193152
  212.6 1.9 copy-start.10
  212.7 311.1 %reduce-scatter.19.cloned.1.call-start = ((), (), s32[]{:S(2)}) async-start(), calls=%async_computation.9 | async-start | bytes 6193152
  225.2 0.7 copy-start.16
  225.2 318.3 %copy-start.12 = (f32[2,224,768]{2,1,0:T(8,128)S(1)}, f32[2,224,768]{2,1,0:T(8,128)}, u32[]{:S(2)}) copy-start(f32[2,224,768]{2,1,0:T(8,128)} %param.10) | copy-start | bytes 4128772
  225.2 378.4 %all-gather.14.cloned.1.call-start = ((), (), s32[]{:S(2)}) async-start(), calls=%async_computation.8 | async-start | bytes 6193152 | tf_op jit(solution)/reshape | solution.py:58
  547.6 4.7 copy-start.13
  547.6 114.6 %all-gather.12.cloned.1.call-start = ((), (), s32[]{:S(2)}) async-start(), calls=%async_computation.7 | async-start | bytes 6193152 | tf_op jit(solution)/reshape | solution.py:58
  552.2 168.6 %all-gather.10.cloned.1.call-start = ((), (), s32[]{:S(2)}) async-start(), calls=%async_computation.6 | async-start | bytes 6193152 | tf_op jit(solution)/reshape | solution.py:58
  720.8 5.9 copy-start.4
  720.8 8.8 %slice-start = ((s8[5505024]{0:T(1024)(128)(4,1)}), s8[4194304]{0:T(1024)(128)(4,1)S(1)}, s32[]{:S(2)}) async-start(s8[5505024]{0:T(1024)(128)(4,1)} %bitcast.347), calls=%async_computation.15 | async-start | bytes 8388608
  726.7 4.0 slice-start.1
Sparse Core Ops, SparseCore 0:
  141.1 64.8 reduce-scatter.28
  208.3 60.9 reduce-scatter.26
  272.2 60.9 reduce-scatter.24
  335.4 60.9 reduce-scatter.22
  399.1 60.9 reduce-scatter.20
  462.8 60.9 reduce-scatter.18
  547.7 55.8 all-gather.13
  605.8 56.3 all-gather.11
  664.4 56.3 all-gather.9
where the time goes:
time: 749 us; the launch traced here: 740 us
  waiting for transfers between devices  454 us (61%)
  matrix products  170 us (23%)
  other arithmetic  50.1 us (7%)
  local copies, waits for them, and re-layouts  32.6 us (4%)
  between operations  17.9 us (2%)
  blocking collectives  15 us (2%)
    unnamed x15, waiting for transfers between devices  289 us
    reshape x3, waiting for transfers between devices, step(): t.reshape(-1, *t.shape[2:])  164 us
    dot_general x5, matrix products, layer(): up = jnp.dot(a, w['w_up'], preferred_element_type=jnp.float32)  63.1 us
    dot_general x5, matrix products, layer(): gate = jnp.dot(a, w['w_gate'], preferred_element_type=jnp.float32)  55.7 us
    dot_general x5, matrix products, matmul(): jnp.dot(a, w, preferred_element_type=jnp.float32).astype(jnp.bfloat16)  51.7 us
    unnamed x49, local copies, waits for them, and re-layouts  32 us
    unnamed x5, other arithmetic  25 us
  transfers between devices with their start and end apart: 9, of which 8 were waited for; matrix products, arithmetic and copies ran while one was open for 13% of the time, Pallas kernels for 0%

commit v1 on v0

v1 whole, which is shorter than its diff:
```python
import functools

import jax
import jax.numpy as jnp
from jax import lax
from jax.experimental import pallas as pl
from jax.experimental.pallas import tpu as pltpu
from jax.sharding import PartitionSpec as P

F32, BF16 = jnp.float32, jnp.bfloat16
MESH = pl.DeviceIdType.MESH
VMEM_LIMIT = 67_043_328
CHUNK = 256


def dot(a, b, ca=1, cb=0):
    return lax.dot_general(a, b, (((ca,), (cb,)), ((), ())), preferred_element_type=F32)


def placed():
    me = lax.axis_index("dp")
    z, c = me // 2, me % 2
    h = z // 2
    end = (z + h) % 2 == 0
    return me, z, c, h, end


def remote(src, dst, send, recv, to):
    return pltpu.make_async_remote_copy(
        src_ref=src, dst_ref=dst, send_sem=send, recv_sem=recv, device_id={"dp": to}, device_id_type=MESH
    )


def gradients_kernel(
    T, D, FF, x_hbm, dy_hbm, wg_hbm, wu_hbm, wd_hbm, gg_ref, gu_ref, gd_ref,
    H, A0, A1, AT, DY, ACC, hid, dg, du, wgs, wus, wds,
    own, prec, fin, RE, RM, ownd, precd, find, REd, RMd,
    w_sem, in_sem, d_send, d_recv, e_send, e_recv, m_send, m_recv,
    dd_send, dd_recv, ed_send, ed_recv, md_send, md_recv,
):
    me, z, c, h, end = placed()
    partner = z * 2 + 1 - c
    d = 1 - 2 * h
    inward, outward = (z + d) * 2 + c, (z - d) * 2 + c
    mid = jnp.logical_not(end)
    TT = min(512, T)
    tiles = T // TT
    steps = FF // CHUNK
    RG, RD = D // 8, FF // 8

    def target(q):
        return q + h * (3 - 2 * q)

    def column(i):
        return (i + steps - 2) % steps

    def rows(t):
        return pl.ds(pl.multiple_of(t * TT, TT), TT)

    def weights(l, i, s):
        cols = pl.ds(pl.multiple_of(column(i) * CHUNK, CHUNK), CHUNK)
        slot = s % 2
        return (
            pltpu.make_async_copy(wg_hbm.at[l, :, cols], wgs.at[slot], w_sem.at[slot, 0]),
            pltpu.make_async_copy(wu_hbm.at[l, :, cols], wus.at[slot], w_sem.at[slot, 1]),
            pltpu.make_async_copy(wd_hbm.at[l, cols, :], wds.at[slot], w_sem.at[slot, 2]),
        )

    get_x = pltpu.make_async_copy(x_hbm, H, in_sem.at[0])
    get_dy = pltpu.make_async_copy(dy_hbm, DY, in_sem.at[1])
    get_x.start()
    for copy in weights(0, 0, 0):
        copy.start()
    get_dy.start()

    barrier = pltpu.get_barrier_semaphore()
    pl.semaphore_signal(barrier, inc=1, device_id={"dp": partner}, device_id_type=MESH)
    pl.semaphore_signal(barrier, inc=1, device_id={"dp": inward}, device_id_type=MESH)

    @pl.when(mid)
    def _():
        pl.semaphore_signal(barrier, inc=1, device_id={"dp": outward}, device_id_type=MESH)
        pl.semaphore_wait(barrier, 3)

    @pl.when(end)
    def _():
        pl.semaphore_wait(barrier, 2)

    def normed(wide):
        return wide * lax.rsqrt(jnp.mean(wide * wide, -1, keepdims=True) + 1e-6)

    get_x.wait()

    def first(t, _):
        A0[rows(t)] = normed(H[rows(t)].astype(F32)).astype(BF16)
        return 0

    lax.fori_loop(0, tiles, first, 0)

    def next_weights(l, i, s, after):
        for copy in weights(l, i, s):
            copy.wait()

        @pl.when(i < steps - 1)
        def _():
            for copy in weights(l, i + 1, s + 1):
                copy.start()

        if after is not None:

            @pl.when(i == steps - 1)
            def _():
                for copy in weights(after, 0, s + 1):
                    copy.start()

    def forward(i, _):
        next_weights(0, i, i, 1)
        slot = i % 2

        def tile(t, _):
            a = A0[rows(t)]
            gate, up = dot(a, wgs[slot]), dot(a, wus[slot])
            hidden = (gate * lax.logistic(gate) * up).astype(BF16)
            down = dot(hidden, wds[slot])

            @pl.when(i == 0)
            def _():
                ACC[rows(t)] = down

            @pl.when(i > 0)
            def _():
                ACC[rows(t)] += down

            return 0

        lax.fori_loop(0, tiles, tile, 0)
        return 0

    lax.fori_loop(0, steps, forward, 0)

    def between(t, _):
        out = ACC[rows(t)].astype(BF16).astype(F32)
        h1 = (H[rows(t)].astype(F32) + out).astype(BF16)
        H[rows(t)] = h1
        a = normed(h1.astype(F32)).astype(BF16)
        A1[rows(t)] = a
        AT[:, rows(t)] = a.T
        return 0

    lax.fori_loop(0, tiles, between, 0)
    get_dy.wait()

    def to_partner(k):
        return remote(own.at[k % 4, :, 1 - c], prec.at[k], d_send.at[k], d_recv.at[k], partner)

    def to_partner_d(p, zt):
        block = pl.ds(pl.multiple_of((2 * zt + 1 - c) * RD, RD), RD)
        return remote(ownd.at[p, block], precd.at[p, zt], dd_send.at[p, zt], dd_recv.at[p, zt], partner)

    def from_end(k, q):
        return remote(prec.at[k, target(q)], RE.at[k, q - 1], e_send.at[k, q - 1], e_recv.at[k, q - 1], inward)

    def across(k, q):
        return remote(prec.at[k, target(q)], RM.at[k, 3 - q], e_send.at[k, q - 1], m_recv.at[k, 3 - q], inward)

    def to_end(k):
        return remote(prec.at[k, target(0)], RM.at[k, 0], m_send.at[k], m_recv.at[k, 0], outward)

    def from_end_d(p, q):
        return remote(precd.at[p, target(q)], REd.at[p, q - 1], ed_send.at[p, q - 1], ed_recv.at[p, q - 1], inward)

    def across_d(p, q):
        return remote(precd.at[p, target(q)], RMd.at[p, 3 - q], ed_send.at[p, q - 1], md_recv.at[p, 3 - q], inward)

    def to_end_d(p):
        return remote(precd.at[p, target(0)], RMd.at[p, 0], md_send.at[p], md_recv.at[p, 0], outward)

    def both(k, zt):
        return own[k % 4, zt, c].astype(F32) + prec[k, zt].astype(F32)

    def both_d(p, zt):
        block = pl.ds(pl.multiple_of((2 * zt + c) * RD, RD), RD)
        return ownd[p, block].astype(F32) + precd[p, zt].astype(F32)

    def share(k):
        to_partner(k).wait()
        fin[k] = both(k, z)

        @pl.when(end)
        def _():
            for q in (3, 2, 1):
                prec[k, target(q)] = both(k, target(q)).astype(BF16)
                from_end(k, q).start()

    def share_d(p, zt):
        to_partner_d(p, zt).wait()
        q = zt + h * (3 - 2 * zt)

        @pl.when(zt == z)
        def _():
            find[p] = both_d(p, zt)

        @pl.when(jnp.logical_and(end, zt != z))
        def _():
            precd[p, zt] = both_d(p, zt).astype(BF16)
            from_end_d(p, q).start()

    def pass_on(k):
        @pl.when(mid)
        def _():
            for q in (3, 2):
                from_end(k, q).wait_recv()
                prec[k, target(q)] = (both(k, target(q)) + RE[k, q - 1].astype(F32)).astype(BF16)
                across(k, q).start()

    def pass_back(k):
        @pl.when(mid)
        def _():
            across(k, 3).wait_recv()
            prec[k, target(0)] = (both(k, target(0)) + RM[k, 0].astype(F32)).astype(BF16)
            to_end(k).start()

    def pass_on_d(p, q):
        @pl.when(mid)
        def _():
            from_end_d(p, q).wait_recv()
            precd[p, target(q)] = (both_d(p, target(q)) + REd[p, q - 1].astype(F32)).astype(BF16)
            across_d(p, q).start()

    def pass_back_d(p):
        @pl.when(mid)
        def _():
            across_d(p, 3).wait_recv()
            precd[p, target(0)] = (both_d(p, target(0)) + RMd[p, 0].astype(F32)).astype(BF16)
            to_end_d(p).start()

    def backward(p, A, i, _):
        l = 1 - p
        s = steps * (1 + p) + i
        k = steps * p + i
        slot = s % 2
        j = column(i)
        next_weights(l, i, s, 0 if p == 0 else None)

        def tile(t, _):
            a = A[rows(t)]
            gate, up = dot(a, wgs[slot]), dot(a, wus[slot])
            dh = dot(DY[rows(t)], wds[slot], 1, 1).astype(BF16).astype(F32)
            sig = lax.logistic(gate)
            act = gate * sig
            hid[rows(t)] = (act * up).astype(BF16)
            du[rows(t)] = (dh * act).astype(BF16)
            dg[rows(t)] = (dh * up * (sig * (1.0 + gate * (1.0 - sig)))).astype(BF16)
            return 0

        lax.fori_loop(0, tiles, tile, 0)
        here = pl.ds(pl.multiple_of(j * CHUNK, CHUNK), CHUNK)
        ownd[p, here] = dot(hid[...], DY[...], 0, 0).astype(BF16)
        zt = (i // 2 + 3) % 4
        down_ready = jnp.logical_or(i % 2 == 1, i == steps - 1)

        @pl.when(down_ready)
        def _():
            to_partner_d(p, zt).start()

        own[k % 4, :, :, 0] = dot(AT[...], dg[...]).astype(BF16).reshape(4, 2, RG, CHUNK)
        own[k % 4, :, :, 1] = dot(AT[...], du[...]).astype(BF16).reshape(4, 2, RG, CHUNK)
        to_partner(k).start()

        if p == 0:

            def back(t, _):
                da = dot(dg[rows(t)], wgs[slot], 1, 1) + dot(du[rows(t)], wus[slot], 1, 1)

                @pl.when(i == 0)
                def _():
                    ACC[rows(t)] = da

                @pl.when(i > 0)
                def _():
                    ACC[rows(t)] += da

                return 0

            lax.fori_loop(0, tiles, back, 0)

        @pl.when(down_ready)
        def _():
            share_d(p, zt)

        share(k)

        @pl.when(k >= 2)
        def _():
            pass_on(k - 2)

        @pl.when(k >= 3)
        def _():
            pass_back(k - 3)

        if p == 1:

            @pl.when(i == 3)
            def _():
                pass_on_d(0, 3)
                pass_on_d(0, 2)
                pass_back_d(0)

        return 0

    lax.fori_loop(0, steps, functools.partial(backward, 0, A1), 0)

    def through_norm(t, _):
        da = ACC[rows(t)].astype(BF16).astype(F32)
        wide = H[rows(t)].astype(F32)
        scale = lax.rsqrt(jnp.mean(wide * wide, -1, keepdims=True) + 1e-6)
        along = jnp.mean(da * wide, -1, keepdims=True)
        dh = (da * scale - wide * (scale * scale * scale * along)).astype(BF16).astype(F32)
        DY[rows(t)] = (DY[rows(t)].astype(F32) + dh).astype(BF16)
        AT[:, rows(t)] = A0[rows(t)].T
        return 0

    lax.fori_loop(0, tiles, through_norm, 0)
    lax.fori_loop(0, steps, functools.partial(backward, 1, A0), 0)

    last = 2 * steps - 1
    pass_on_d(1, 3)
    pass_on(last - 1)
    pass_on_d(1, 2)
    pass_on(last)
    pass_back_d(1)
    pass_back(last - 2)
    pass_back(last - 1)
    pass_back(last)

    def finish(k, _):
        p, i = k // steps, k % steps
        l = 1 - p
        cols = pl.ds(pl.multiple_of(column(i) * CHUNK, CHUNK), CHUNK)

        def put(total):
            gg_ref[l, :, cols] = total[0].astype(BF16)
            gu_ref[l, :, cols] = total[1].astype(BF16)

        @pl.when(end)
        def _():
            to_end(k).wait_recv()
            put(fin[k] + RM[k, 0].astype(F32))

        @pl.when(mid)
        def _():
            from_end(k, 1).wait_recv()
            across(k, 2).wait_recv()
            put(fin[k] + RE[k, 0].astype(F32) + RM[k, 1].astype(F32))

        return 0

    def finish_d(p):
        @pl.when(end)
        def _():
            to_end_d(p).wait_recv()
            gd_ref[1 - p] = (find[p] + RMd[p, 0].astype(F32)).astype(BF16)

        @pl.when(mid)
        def _():
            from_end_d(p, 1).wait_recv()
            across_d(p, 2).wait_recv()
            gd_ref[1 - p] = (find[p] + REd[p, 0].astype(F32) + RMd[p, 1].astype(F32)).astype(BF16)

    finish_d(0)
    finish_d(1)
    lax.fori_loop(0, 2 * steps, finish, 0)

    def sent(k, _):
        @pl.when(end)
        def _():
            for q in (3, 2, 1):
                from_end(k, q).wait_send()

        @pl.when(mid)
        def _():
            across(k, 3).wait_send()
            across(k, 2).wait_send()
            to_end(k).wait_send()

        return 0

    lax.fori_loop(0, 2 * steps, sent, 0)
    for p in range(2):

        @pl.when(end)
        def _():
            for q in (3, 2, 1):
                from_end_d(p, q).wait_send()

        @pl.when(mid)
        def _():
            across_d(p, 3).wait_send()
            across_d(p, 2).wait_send()
            to_end_d(p).wait_send()


def gradients(x, dy, wg, wu, wd):
    T, D = x.shape
    L, _, FF = wg.shape
    n = L * (FF // CHUNK)
    RG, RD = D // 8, FF // 8
    V, DMA = pltpu.VMEM, pltpu.SemaphoreType.DMA
    piece = (2, RG, CHUNK)
    return pl.pallas_call(
        functools.partial(gradients_kernel, T, D, FF),
        out_shape=[
            jax.ShapeDtypeStruct((L, RG, FF), BF16),
            jax.ShapeDtypeStruct((L, RG, FF), BF16),
            jax.ShapeDtypeStruct((L, RD, D), BF16),
        ],
        in_specs=[pl.BlockSpec(memory_space=pl.ANY)] * 5,
        out_specs=[pl.BlockSpec(memory_space=pltpu.VMEM)] * 3,
        scratch_shapes=[
            V((T, D), BF16), V((T, D), BF16), V((T, D), BF16), V((D, T), BF16), V((T, D), BF16), V((T, D), F32),
            V((T, CHUNK), BF16), V((T, CHUNK), BF16), V((T, CHUNK), BF16),
            V((2, D, CHUNK), BF16), V((2, D, CHUNK), BF16), V((2, CHUNK, D), BF16),
            V((4, 4, 2, *piece), BF16), V((n, 4, *piece), BF16), V((n, *piece), F32),
            V((n, 3, *piece), BF16), V((n, 2, *piece), BF16),
            V((L, FF, D), BF16), V((L, 4, RD, D), BF16), V((L, RD, D), F32),
            V((L, 3, RD, D), BF16), V((L, 2, RD, D), BF16),
            DMA((2, 3)), DMA((2,)), DMA((n,)), DMA((n,)), DMA((n, 3)), DMA((n, 3)), DMA((n,)), DMA((n, 2)),
            DMA((L, 4)), DMA((L, 4)), DMA((L, 3)), DMA((L, 3)), DMA((L,)), DMA((L, 2)),
        ],
        compiler_params=pltpu.CompilerParams(collective_id=0, has_side_effects=True, vmem_limit_bytes=VMEM_LIMIT),
        name="gradients",
    )(x, dy, wg, wu, wd)


def update_kernel(count, *refs):
    g_hbm, m_hbm, v_hbm, w_hbm = refs[0:3], refs[3:6], refs[6:9], refs[9:12]
    w_out, m_out, v_out = refs[12:15], refs[15:18], refs[18:21]
    g_s, m_s, v_s, w_s, n_s = refs[21:24], refs[24:27], refs[27:30], refs[30:33], refs[33:36]
    sq, in_sem, sq_send, sq_recv, r_send, r_recv, l_send, l_recv, p_send, p_recv, own_sem, mv_sem = refs[36:]
    me, z, c, h, end = placed()
    partner = z * 2 + 1 - c
    L = 2
    parts = [(l, t) for l in (1, 0) for t in (2, 0, 1)]

    loads = []
    for t in range(3):
        block = pl.ds(pl.multiple_of(me * g_s[t].shape[1], 32), g_s[t].shape[1])
        loads.append([
            pltpu.make_async_copy(g_hbm[t], g_s[t], in_sem.at[t, 0]),
            pltpu.make_async_copy(m_hbm[t], m_s[t], in_sem.at[t, 1]),
            pltpu.make_async_copy(v_hbm[t], v_s[t], in_sem.at[t, 2]),
            pltpu.make_async_copy(w_hbm[t].at[:, block], w_s[t], in_sem.at[t, 3]),
        ])
    for which in range(4):
        for t in (2, 0, 1):
            loads[t][which].start()

    barrier = pltpu.get_barrier_semaphore()
    for other in range(1, 8):
        pl.semaphore_signal(barrier, inc=1, device_id={"dp": (me + other) % 8}, device_id_type=MESH)

    STEP = 16

    def strip(r):
        return pl.ds(pl.multiple_of(r * STEP, STEP), STEP)

    total = jnp.zeros((8, 128), F32)
    for t in range(3):
        loads[t][0].wait()
        R, C = g_s[t].shape[1:]

        def squares(r, total, t=t, R=R, C=C):
            l, q = r // (R // STEP), r % (R // STEP)
            g = g_s[t][l, strip(q)].astype(F32)
            return total + jnp.sum((g * g).reshape(STEP // 8, 8, C // 128, 128), axis=(0, 2))

        total = lax.fori_loop(0, L * (R // STEP), squares, total)
    sq[me] = total
    pl.semaphore_wait(barrier, 7)

    def tell(other):
        to = (me + other) % 8
        return remote(sq.at[me], sq.at[me], sq_send.at[other], sq_recv.at[8 - other], to)

    def told(other):
        src = (me + other) % 8
        return remote(sq.at[src], sq.at[src], sq_send.at[8 - other], sq_recv.at[other], me)

    for other in range(1, 8):
        tell(other).start()
    for t in range(3):
        for which in (1, 2, 3):
            loads[t][which].wait()
    for other in range(1, 8):
        told(other).wait_recv()
    for other in range(1, 8):
        tell(other).wait_send()
    whole = jnp.full((8, 128), jnp.sum(sq[...]), F32)
    factor = jnp.minimum(1.0, 0.5 * lax.rsqrt(whole / count + 1e-30))[0:1, 0:1]

    def block(p, zt, ct):
        l, t = parts[p]
        R = g_s[t].shape[1]
        return w_out[t].at[l, pl.ds(pl.multiple_of((2 * zt + ct) * R, 32), R)]

    def mine(p):
        l, t = parts[p]
        return n_s[t].at[l]

    def to_right(p, hop):
        src = mine(p) if hop == 0 else block(p, z - hop, c)
        return remote(src, block(p, z - hop, c), r_send.at[p, hop], r_recv.at[p, hop], (z + 1) * 2 + c)

    def to_left(p, hop):
        src = mine(p) if hop == 0 else block(p, z + hop, c)
        return remote(src, block(p, z + hop, c), l_send.at[p, hop], l_recv.at[p, hop], (z - 1) * 2 + c)

    def to_partner(p, zt, own=False):
        return remote(mine(p) if own else block(p, zt, c), block(p, zt, c), p_send.at[p, zt], p_recv.at[p, zt], partner)

    def keep(p):
        return pltpu.make_async_copy(mine(p), block(p, z, c), own_sem.at[p])

    def moments(p):
        l, t = parts[p]
        return (
            pltpu.make_async_copy(m_s[t].at[l], m_out[t].at[l], mv_sem.at[p, 0]),
            pltpu.make_async_copy(v_s[t].at[l], v_out[t].at[l], mv_sem.at[p, 1]),
        )

    for p, (l, t) in enumerate(parts):

        def adamw(r, _, l=l, t=t):
            at = strip(r)
            g = g_s[t][l, at].astype(F32) * factor
            w = w_s[t][l, at].astype(F32)
            m = 0.9 * m_s[t][l, at] + 0.1 * g
            v = 0.95 * v_s[t][l, at] + 0.05 * g * g
            m_s[t][l, at] = m
            v_s[t][l, at] = v
            n_s[t][l, at] = (w - 0.02 * (m * lax.rsqrt(v + 1e-8) + 0.1 * w)).astype(BF16)
            return 0

        lax.fori_loop(0, g_s[t].shape[1] // STEP, adamw, 0)

        @pl.when(z < 3)
        def _():
            to_right(p, 0).start()

        @pl.when(z > 0)
        def _():
            to_left(p, 0).start()

        to_partner(p, z, True).start()
        keep(p).start()
        for copy in moments(p):
            copy.start()

    n = len(parts)
    for hop in range(3):
        for p in range(n):

            @pl.when(z > hop)
            def _():
                to_right(p, hop).wait_recv()

                if hop < 2:

                    @pl.when(z < 3)
                    def _():
                        to_right(p, hop + 1).start()

                to_partner(p, z - hop - 1).start()

            @pl.when(z + hop < 3)
            def _():
                to_left(p, hop).wait_recv()

                if hop < 2:

                    @pl.when(z > 0)
                    def _():
                        to_left(p, hop + 1).start()

                to_partner(p, z + hop + 1).start()

    for p in range(n):
        for zt in range(4):
            to_partner(p, zt).wait_recv()
    for p in range(n):
        keep(p).wait()
        for copy in moments(p):
            copy.wait()
        for zt in range(4):
            to_partner(p, zt).wait_send()
        for hop in range(3):

            @pl.when(jnp.logical_and(z < 3, z >= hop))
            def _():
                to_right(p, hop).wait_send()

            @pl.when(jnp.logical_and(z > 0, z + hop <= 3))
            def _():
                to_left(p, hop).wait_send()


def update(g, m, v, w):
    V, DMA = pltpu.VMEM, pltpu.SemaphoreType.DMA
    S = jax.ShapeDtypeStruct
    count = 8 * sum(a.size for a in g)
    out = [S(a.shape, BF16) for a in w] + [S(a.shape, F32) for a in (*m, *v)]
    return pl.pallas_call(
        functools.partial(update_kernel, float(count)),
        out_shape=out,
        in_specs=[pl.BlockSpec(memory_space=pl.ANY)] * 12,
        out_specs=[pl.BlockSpec(memory_space=pl.ANY)] * 9,
        scratch_shapes=[
            *(V(a.shape, BF16) for a in g), *(V(a.shape, F32) for a in m), *(V(a.shape, F32) for a in v),
            *(V(a.shape, BF16) for a in g), *(V(a.shape, BF16) for a in g),
            V((8, 8, 128), F32), DMA((3, 4)), DMA((8,)), DMA((8,)),
            DMA((6, 3)), DMA((6, 3)), DMA((6, 3)), DMA((6, 3)), DMA((6, 4)), DMA((6, 4)), DMA((6,)), DMA((6, 2)),
        ],
        compiler_params=pltpu.CompilerParams(collective_id=1, has_side_effects=True, vmem_limit_bytes=VMEM_LIMIT),
        name="update",
    )(*g, *m, *v, *w)


def solution(mesh):
    def step(x, dy, *arrays):
        w, m, v = (arrays[i : i + 3] for i in (0, 3, 6))
        g = gradients(x[0], dy[0], *w)
        return tuple(update(g, m, v, w))

    whole, split = P(None, None, None), P(None, "dp", None)
    return jax.shard_map(
        step,
        mesh=mesh,
        in_specs=(P(("rep", "dp")),) * 2 + (whole,) * 3 + (split,) * 6,
        out_specs=(P("rep", None, None),) * 3 + (P("rep", "dp", None),) * 6,
        check_vma=False,
    )
```

time: 749 us -> 383 us (0.51); the launches traced: 740 us -> 383 us
  waiting for transfers between devices: 454 us -> 0 us
  Pallas kernels: 0 us -> 359 us
  matrix products: 170 us -> 0 us
  other arithmetic: 50.1 us -> 0 us
  between operations: 17.9 us -> 0.68 us
  blocking collectives: 15 us -> 0 us
  local copies, waits for them, and re-layouts: 32.6 us -> 22.8 us
    pallas_call x0 -> x2, Pallas kernels: none -> 359 us  [the longest x1 214 us: gradients(): pl.pallas_call(functools.partial(gradients_kernel, T, D, FF), out_shape=[...]
    unnamed x15 -> x0, waiting for transfers between devices: 289 us -> none
    dot_general x15 -> x0, matrix products: 170 us -> none  [the longest x5 63.1 us: layer(): up = jnp.dot(a, w['w_up'], preferred_element_type=jnp.float32)]
    reshape x3 -> x0, waiting for transfers between devices: 164 us -> none  [step(): t.reshape(-1, *t.shape[2:])]
    unnamed x5 -> x0, other arithmetic: 25 us -> none
    reduce_sum x1 -> x0, blocking collectives: 15 us -> none  [of_a_group(): jnp.sum(g * g)]
    reshape x3 -> x0, other arithmetic: 12.7 us -> none  [step(): t.reshape(-1, *t.shape[2:])]
    unnamed x49 -> x25, local copies, waits for them, and re-layouts: 32 us -> 22.8 us
  transfers between devices with their start and end apart: 9 -> 0, of which waited for: 8 -> 0; matrix products, arithmetic and copies ran while one was open for 13% -> 0% of each run, Pallas kernels for 0% -> 0%
where the time goes in v1:
time: 383 us
  Pallas kernels  359 us (94%)
  local copies, waits for them, and re-layouts  22.8 us (6%)
    pallas_call x1, Pallas kernels, gradients(): pl.pallas_call(functools.partial(gradients_kernel, T, D, FF), out_shape=[...  214 us
    pallas_call x1, Pallas kernels, update(): pl.pallas_call(functools.partial(update_kernel, float(count)), out_shape=...  146 us
    unnamed x25, local copies, waits for them, and re-layouts  22.8 us

profile of v1, /device:TPU:0, one launch (start us, length us, event | category | flops | bytes accessed | tf_op | source)
XLA Modules:
  0.0 382.9 jit_solution(7534961364097617747)
XLA Ops:
  0.6 213.7 %gradients.1 = (bf16[2,96,1792]{2,1,0:T(8,128)(2,1)}, bf16[2,96,1792]{2,1,0:T(8,128)(2,1)}, bf16[2,224,768]{2,1,0:T(8,128)(2,1)}) custom-call(bf16[2048,768]{1,0:T(8,128)(2,1)} %bitcast.2, bf16[2048,768]{1,0:T(8,128)(2,1)} %bitcast.3, bf16[2,768,1792]{2,1,0:T(8,128)(2,1)} %refs_9_.1, bf16[2,768,1792]{2,1,0:T(8,128)(2,1)} %refs_10_.1, ...), custom_call_target="tpu_custom_call" | custom-call | tf_op jit(solution)/shard_map/gradients/pallas_call | solution.py:410
  214.3 145.8 %update.1 = (bf16[2,768,1792]{2,1,0:T(8,128)(2,1)}, bf16[2,768,1792]{2,1,0:T(8,128)(2,1)}, bf16[2,1792,768]{2,1,0:T(8,128)(2,1)}, f32[2,96,1792]{2,1,0:T(8,128)}...) custom-call(bf16[2,96,1792]{2,1,0:T(8,128)(2,1)} %get-tuple-element., ...), custom_call_target="tpu_custom_call" | custom-call | tf_op jit(solution)/shard_map/update/pallas_call | solution.py:612
  360.1 0.0 copy-start.1
  360.1 5.5 %copy.29 = bf16[2,768,1792]{2,1,0:T(8,128)(2,1)} copy(bf16[2,768,1792]{2,1,0:T(8,128)(2,1)} %get-tuple-element.24) | data formatting | bytes 11010048
  365.6 0.0 copy-done.1
  365.6 0.0 copy-start
  365.6 2.8 copy.30
  368.4 1.7 copy-done
  370.2 0.0 copy-start.7
  370.2 2.4 copy.31
  372.6 0.0 copy-done.7
  372.6 0.0 copy-start.6
  372.6 1.1 copy.32
  373.7 0.8 copy-done.6
  374.5 0.0 copy-start.5
  374.5 1.1 copy.33
  375.5 0.8 copy-done.5
  376.3 0.0 copy-start.4
  376.3 1.1 copy.34
  377.4 0.8 copy-done.4
  378.1 0.0 copy-start.3
  378.1 1.1 copy.35
  379.2 0.8 copy-done.3
  380.0 0.0 copy-start.2
  380.0 1.1 copy.36
  381.1 0.8 copy-done.2
  381.8 1.1 copy.37
Async XLA Ops:
  360.1 5.5 %copy-start.1 = (bf16[2,768,1792]{2,1,0:T(8,128)(2,1)S(1)}, bf16[2,768,1792]{2,1,0:T(8,128)(2,1)}, u32[]{:S(2)}) copy-start(bf16[2,768,1792]{2,1,0:T(8,128)(2,1)} %get-tuple-element.25) | copy-start | bytes 16515076
  365.6 4.5 %copy-start = (bf16[2,1792,768]{2,1,0:T(8,128)(2,1)S(1)}, bf16[2,1792,768]{2,1,0:T(8,128)(2,1)}, u32[]{:S(2)}) copy-start(bf16[2,1792,768]{2,1,0:T(8,128)(2,1)} %get-tuple-element.26) | copy-start | bytes 16515076
  370.2 2.4 copy-start.7
  372.6 1.8 copy-start.6
  374.5 1.8 copy-start.5
  376.3 1.8 copy-start.4
  378.1 1.8 copy-start.3
  380.0 1.8 copy-start.2

commit v2 on v1

--- a/solution.py
+++ b/solution.py
@@ -93,6 +93,7 @@
 
     def first(t, _):
         A0[rows(t)] = normed(H[rows(t)].astype(F32)).astype(BF16)
+        ACC[rows(t)] = jnp.zeros((TT, D), F32)
         return 0
 
     lax.fori_loop(0, tiles, first, 0)
@@ -123,14 +124,7 @@
             hidden = (gate * lax.logistic(gate) * up).astype(BF16)
             down = dot(hidden, wds[slot])
 
-            @pl.when(i == 0)
-            def _():
-                ACC[rows(t)] = down
-
-            @pl.when(i > 0)
-            def _():
-                ACC[rows(t)] += down
-
+            ACC[rows(t)] += down
             return 0
 
         lax.fori_loop(0, tiles, tile, 0)
@@ -140,6 +134,7 @@
 
     def between(t, _):
         out = ACC[rows(t)].astype(BF16).astype(F32)
+        ACC[rows(t)] = jnp.zeros((TT, D), F32)
         h1 = (H[rows(t)].astype(F32) + out).astype(BF16)
         H[rows(t)] = h1
         a = normed(h1.astype(F32)).astype(BF16)
@@ -271,15 +266,7 @@
 
             def back(t, _):
                 da = dot(dg[rows(t)], wgs[slot], 1, 1) + dot(du[rows(t)], wus[slot], 1, 1)
-
-                @pl.when(i == 0)
-                def _():
-                    ACC[rows(t)] = da
-
-                @pl.when(i > 0)
-                def _():
-                    ACC[rows(t)] += da
-
+                ACC[rows(t)] += da
                 return 0
 
             lax.fori_loop(0, tiles, back, 0)
@@ -612,7 +599,7 @@
     return pl.pallas_call(
         functools.partial(update_kernel, float(count)),
         out_shape=out,
-        in_specs=[pl.BlockSpec(memory_space=pl.ANY)] * 12,
+        in_specs=[pl.BlockSpec(memory_space=pltpu.HBM)] * 12,
         out_specs=[pl.BlockSpec(memory_space=pl.ANY)] * 9,
         scratch_shapes=[
             *(V(a.shape, BF16) for a in g), *(V(a.shape, F32) for a in m), *(V(a.shape, F32) for a in v),
@@ -620,16 +607,39 @@
             V((8, 8, 128), F32), DMA((3, 4)), DMA((8,)), DMA((8,)),
             DMA((6, 3)), DMA((6, 3)), DMA((6, 3)), DMA((6, 3)), DMA((6, 4)), DMA((6, 4)), DMA((6,)), DMA((6, 2)),
         ],
-        compiler_params=pltpu.CompilerParams(collective_id=1, has_side_effects=True, vmem_limit_bytes=VMEM_LIMIT),
+        compiler_params=pltpu.CompilerParams(collective_id=1, has_side_effects=True, vmem_limit_bytes=18_000_000),
         name="update",
     )(*g, *m, *v, *w)
+
+
+def store_kernel(*refs):
+    n = len(refs) // 2
+    src, dst, sem = refs[:n], refs[n : 2 * n], refs[2 * n]
+    copies = [pltpu.make_async_copy(src[i].at[l], dst[i].at[l], sem.at[i, l]) for i in range(n) for l in range(2)]
+    for copy in copies:
+        copy.start()
+    for copy in copies:
+        copy.wait()
+
+
+def store(arrays):
+    n = len(arrays)
+    return pl.pallas_call(
+        store_kernel,
+        out_shape=[jax.ShapeDtypeStruct(a.shape, a.dtype) for a in arrays],
+        in_specs=[pl.BlockSpec(memory_space=pl.ANY)] * n,
+        out_specs=[pl.BlockSpec(memory_space=pltpu.HBM)] * n,
+        scratch_shapes=[pltpu.SemaphoreType.DMA((n, 2))],
+        compiler_params=pltpu.CompilerParams(vmem_limit_bytes=1_000_000),
+        name="store",
+    )(*arrays)
 
 
 def solution(mesh):
     def step(x, dy, *arrays):
         w, m, v = (arrays[i : i + 3] for i in (0, 3, 6))
         g = gradients(x[0], dy[0], *w)
-        return tuple(update(g, m, v, w))
+        return tuple(store(update(g, m, v, w)))
 
     whole, split = P(None, None, None), P(None, "dp", None)
     return jax.shard_map(

time: 383 us -> 375 us (0.979)
  local copies, waits for them, and re-layouts: 22.8 us -> 11.3 us
    unnamed x25 -> x18, local copies, waits for them, and re-layouts: 22.8 us -> 11.3 us
    pallas_call x0 -> x1, Pallas kernels: none -> 8.41 us  [store(): pl.pallas_call(store_kernel, out_shape=[jax.ShapeDtypeStruct(a.shape, a.d...]
    pallas_call x1, Pallas kernels: 214 us -> 206 us  [gradients(): pl.pallas_call(functools.partial(gradients_kernel, T, D, FF), out_shape=[...]
where the time goes in v2:
time: 375 us
  Pallas kernels  362 us (97%)
  local copies, waits for them, and re-layouts  11.3 us (3%)
    pallas_call x1, Pallas kernels, gradients(): pl.pallas_call(functools.partial(gradients_kernel, T, D, FF), out_shape=[...  206 us
    pallas_call x1, Pallas kernels, update(): pl.pallas_call(functools.partial(update_kernel, float(count)), out_shape=...  148 us
    unnamed x18, local copies, waits for them, and re-layouts  11.3 us
    pallas_call x1, Pallas kernels, store(): pl.pallas_call(store_kernel, out_shape=[jax.ShapeDtypeStruct(a.shape, a.d...  8.41 us

profile of v2, /device:TPU:0, one launch (start us, length us, event | category | flops | bytes accessed | tf_op | source)
XLA Modules:
  0.0 374.6 jit_solution(8111401126588119993)
XLA Ops:
  0.6 206.2 %gradients.1 = (bf16[2,96,1792]{2,1,0:T(8,128)(2,1)}, bf16[2,96,1792]{2,1,0:T(8,128)(2,1)}, bf16[2,224,768]{2,1,0:T(8,128)(2,1)}) custom-call(bf16[2048,768]{1,0:T(8,128)(2,1)} %bitcast.2, bf16[2048,768]{1,0:T(8,128)(2,1)} %bitcast.3, bf16[2,768,1792]{2,1,0:T(8,128)(2,1)} %refs_9_.1, bf16[2,768,1792]{2,1,0:T(8,128)(2,1)} %refs_10_.1, ...), custom_call_target="tpu_custom_call" | custom-call | tf_op jit(solution)/shard_map/gradients/pallas_call | solution.py:397
  206.9 0.0 copy-start
  206.9 1.3 copy-done
  208.2 0.0 copy-start.1
  208.2 1.3 copy-done.1
  209.5 0.0 copy-start.2
  209.5 1.3 copy-done.2
  210.9 0.0 copy-start.3
  210.9 1.3 copy-done.3
  212.2 0.0 copy-start.4
  212.2 1.3 copy-done.4
  213.6 0.0 copy-start.5
  213.6 1.3 copy-done.5
  214.9 0.0 copy-start.6
  214.9 1.1 copy-done.6
  216.0 0.0 copy-start.7
  216.0 1.1 copy-done.7
  217.1 0.0 copy-start.8
  217.1 1.1 copy-done.8
  218.2 147.8 %update.1 = (bf16[2,768,1792]{2,1,0:T(8,128)(2,1)S(1)}, bf16[2,768,1792]{2,1,0:T(8,128)(2,1)S(1)}, bf16[2,1792,768]{2,1,0:T(8,128)(2,1)S(1)}, f32[2,96,1792]{2,1...) custom-call(bf16[2,96,1792]{2,1,0:T(8,128)(2,1)S(1)} %copy-done.6, ...), custom_call_target="tpu_custom_call" | custom-call | tf_op jit(solution)/shard_map/update/pallas_call | solution.py:599
  366.0 8.4 %store.1 = (bf16[2,768,1792]{2,1,0:T(8,128)(2,1)}, bf16[2,768,1792]{2,1,0:T(8,128)(2,1)}, bf16[2,1792,768]{2,1,0:T(8,128)(2,1)}, f32[2,96,1792]{2,1,0:T(8,128)},...) custom-call(bf16[2,768,1792]{2,1,0:T(8,128)(2,1)S(1)} %get-tuple-ele, ...), custom_call_target="tpu_custom_call" | custom-call | tf_op jit(solution)/shard_map/store/pallas_call | solution.py:627
Async XLA Ops:
  206.9 1.3 copy-start
  208.2 1.3 copy-start.1
  209.5 1.3 copy-start.2
  210.9 1.3 copy-start.3
  212.2 1.3 copy-start.4
  213.6 1.3 copy-start.5
  214.9 1.1 copy-start.6
  216.0 1.1 copy-start.7
  217.1 1.1 copy-start.8

commit v3 on v2

--- a/solution.py
+++ b/solution.py
@@ -32,12 +32,15 @@
 
 
 def gradients_kernel(
-    T, D, FF, x_hbm, dy_hbm, wg_hbm, wu_hbm, wd_hbm, gg_ref, gu_ref, gd_ref,
+    T, D, FF, x_hbm, dy_hbm, wg_hbm, wu_hbm, wd_hbm, *refs
+):
+    moments, (gg_ref, gu_ref, gd_ref), lent = refs[:6], refs[6:9], refs[9:18]
+    (
     H, A0, A1, AT, DY, ACC, hid, dg, du, wgs, wus, wds,
     own, prec, fin, RE, RM, ownd, precd, find, REd, RMd,
     w_sem, in_sem, d_send, d_recv, e_send, e_recv, m_send, m_recv,
-    dd_send, dd_recv, ed_send, ed_recv, md_send, md_recv,
-):
+    dd_send, dd_recv, ed_send, ed_recv, md_send, md_recv, lend_send, lend_recv,
+    ) = refs[18:]
     me, z, c, h, end = placed()
     partner = z * 2 + 1 - c
     d = 1 - 2 * h
@@ -80,11 +83,10 @@
     @pl.when(mid)
     def _():
         pl.semaphore_signal(barrier, inc=1, device_id={"dp": outward}, device_id_type=MESH)
-        pl.semaphore_wait(barrier, 3)
-
-    @pl.when(end)
-    def _():
-        pl.semaphore_wait(barrier, 2)
+
+    def lend(n):
+        src = moments[n].at[1] if n < 6 else (gg_ref, gu_ref, gd_ref)[n - 6].at[1]
+        return remote(src, lent[n], lend_send.at[n], lend_recv.at[n], outward)
 
     def normed(wide):
         return wide * lax.rsqrt(jnp.mean(wide * wide, -1, keepdims=True) + 1e-6)
@@ -97,6 +99,17 @@
         return 0
 
     lax.fori_loop(0, tiles, first, 0)
+
+    @pl.when(mid)
+    def _():
+        pl.semaphore_wait(barrier, 3)
+        for n in range(6):
+            lend(n).start()
+
+    @pl.when(end)
+    def _():
+        pl.semaphore_wait(barrier, 2)
+
 
     def next_weights(l, i, s, after):
         for copy in weights(l, i, s):
@@ -228,6 +241,40 @@
             across_d(p, 3).wait_recv()
             precd[p, target(0)] = (both_d(p, target(0)) + RMd[p, 0].astype(F32)).astype(BF16)
             to_end_d(p).start()
+
+    def finish(k, _):
+        p, i = k // steps, k % steps
+        l = 1 - p
+        cols = pl.ds(pl.multiple_of(column(i) * CHUNK, CHUNK), CHUNK)
+
+        def put(total):
+            gg_ref[l, :, cols] = total[0].astype(BF16)
+            gu_ref[l, :, cols] = total[1].astype(BF16)
+
+        @pl.when(end)
+        def _():
+            to_end(k).wait_recv()
+            put(fin[k] + RM[k, 0].astype(F32))
+
+        @pl.when(mid)
+        def _():
+            from_end(k, 1).wait_recv()
+            across(k, 2).wait_recv()
+            put(fin[k] + RE[k, 0].astype(F32) + RM[k, 1].astype(F32))
+
+        return 0
+
+    def finish_d(p):
+        @pl.when(end)
+        def _():
+            to_end_d(p).wait_recv()
+            gd_ref[1 - p] = (find[p] + RMd[p, 0].astype(F32)).astype(BF16)
+
+        @pl.when(mid)
+        def _():
+            from_end_d(p, 1).wait_recv()
+            across_d(p, 2).wait_recv()
+            gd_ref[1 - p] = (find[p] + REd[p, 0].astype(F32) + RMd[p, 1].astype(F32)).astype(BF16)
 
     def backward(p, A, i, _):
         l = 1 - p
@@ -293,6 +340,13 @@
                 pass_on_d(0, 2)
                 pass_back_d(0)
 
+            @pl.when(jnp.logical_and(mid, i == 5))
+            def _():
+                finish_d(0)
+                lax.fori_loop(0, steps, finish, 0)
+                for n in range(6, 9):
+                    lend(n).start()
+
         return 0
 
     lax.fori_loop(0, steps, functools.partial(backward, 0, A1), 0)
@@ -320,43 +374,24 @@
     pass_back(last - 1)
     pass_back(last)
 
-    def finish(k, _):
-        p, i = k // steps, k % steps
-        l = 1 - p
-        cols = pl.ds(pl.multiple_of(column(i) * CHUNK, CHUNK), CHUNK)
-
-        def put(total):
-            gg_ref[l, :, cols] = total[0].astype(BF16)
-            gu_ref[l, :, cols] = total[1].astype(BF16)
+    @pl.when(end)
+    def _():
+        finish_d(0)
+        lax.fori_loop(0, steps, finish, 0)
+
+    finish_d(1)
+    lax.fori_loop(steps, 2 * steps, finish, 0)
+
+    for n in range(9):
 
         @pl.when(end)
         def _():
-            to_end(k).wait_recv()
-            put(fin[k] + RM[k, 0].astype(F32))
-
-        @pl.when(mid)
-        def _():
-            from_end(k, 1).wait_recv()
-            across(k, 2).wait_recv()
-            put(fin[k] + RE[k, 0].astype(F32) + RM[k, 1].astype(F32))
-
-        return 0
-
-    def finish_d(p):
-        @pl.when(end)
-        def _():
-            to_end_d(p).wait_recv()
-            gd_ref[1 - p] = (find[p] + RMd[p, 0].astype(F32)).astype(BF16)
-
-        @pl.when(mid)
-        def _():
-            from_end_d(p, 1).wait_recv()
-            across_d(p, 2).wait_recv()
-            gd_ref[1 - p] = (find[p] + REd[p, 0].astype(F32) + RMd[p, 1].astype(F32)).astype(BF16)
-
-    finish_d(0)
-    finish_d(1)
-    lax.fori_loop(0, 2 * steps, finish, 0)
+            lend(n).wait_recv()
+
+        @pl.when(mid)
+        def _():
+            lend(n).wait_send()
+
 
     def sent(k, _):
         @pl.when(end)
@@ -387,7 +422,7 @@
             to_end_d(p).wait_send()
 
 
-def gradients(x, dy, wg, wu, wd):
+def gradients(x, dy, wg, wu, wd, moments):
     T, D = x.shape
     L, _, FF = wg.shape
     n = L * (FF // CHUNK)
@@ -400,9 +435,11 @@
             jax.ShapeDtypeStruct((L, RG, FF), BF16),
             jax.ShapeDtypeStruct((L, RG, FF), BF16),
             jax.ShapeDtypeStruct((L, RD, D), BF16),
+            *(pltpu.HBM(a.shape[1:], F32) for a in moments),
+            *(pltpu.HBM(a.shape[1:], BF16) for a in moments[:3]),
         ],
-        in_specs=[pl.BlockSpec(memory_space=pl.ANY)] * 5,
-        out_specs=[pl.BlockSpec(memory_space=pltpu.VMEM)] * 3,
+        in_specs=[pl.BlockSpec(memory_space=pl.ANY)] * 11,
+        out_specs=[pl.BlockSpec(memory_space=pltpu.VMEM)] * 3 + [pl.BlockSpec(memory_space=pltpu.HBM)] * 9,
         scratch_shapes=[
             V((T, D), BF16), V((T, D), BF16), V((T, D), BF16), V((D, T), BF16), V((T, D), BF16), V((T, D), F32),
             V((T, CHUNK), BF16), V((T, CHUNK), BF16), V((T, CHUNK), BF16),
@@ -412,22 +449,24 @@
             V((L, FF, D), BF16), V((L, 4, RD, D), BF16), V((L, RD, D), F32),
             V((L, 3, RD, D), BF16), V((L, 2, RD, D), BF16),
             DMA((2, 3)), DMA((2,)), DMA((n,)), DMA((n,)), DMA((n, 3)), DMA((n, 3)), DMA((n,)), DMA((n, 2)),
-            DMA((L, 4)), DMA((L, 4)), DMA((L, 3)), DMA((L, 3)), DMA((L,)), DMA((L, 2)),
+            DMA((L, 4)), DMA((L, 4)), DMA((L, 3)), DMA((L, 3)), DMA((L,)), DMA((L, 2)), DMA((9,)), DMA((9,)),
         ],
         compiler_params=pltpu.CompilerParams(collective_id=0, has_side_effects=True, vmem_limit_bytes=VMEM_LIMIT),
         name="gradients",
-    )(x, dy, wg, wu, wd)
+    )(x, dy, wg, wu, wd, *moments)
 
 
 def update_kernel(count, *refs):
-    g_hbm, m_hbm, v_hbm, w_hbm = refs[0:3], refs[3:6], refs[6:9], refs[9:12]
-    w_out, m_out, v_out = refs[12:15], refs[15:18], refs[18:21]
-    g_s, m_s, v_s, w_s, n_s = refs[21:24], refs[24:27], refs[27:30], refs[30:33], refs[33:36]
-    sq, in_sem, sq_send, sq_recv, r_send, r_recv, l_send, l_recv, p_send, p_recv, own_sem, mv_sem = refs[36:]
+    g_hbm, m_hbm, v_hbm, w_hbm, lent = refs[0:3], refs[3:6], refs[6:9], refs[9:12], refs[12:21]
+    w_out, m_out, v_out, refs = refs[21:24], refs[24:27], refs[27:30], refs[30:]
+    g_s, m_s, v_s, w_s, n_s = refs[0:3], refs[3:6], refs[6:9], refs[9:12], refs[12:15]
+    g_n, m_n, v_n, w_n, n_n, refs = refs[15:18], refs[18:21], refs[21:24], refs[24:27], refs[27:30], refs[30:]
+    sq, in_sem, sq_send, sq_recv, r_send, r_recv, l_send, l_recv, p_send, p_recv, own_sem, mv_sem, near_sem = refs
     me, z, c, h, end = placed()
     partner = z * 2 + 1 - c
     L = 2
-    parts = [(l, t) for l in (1, 0) for t in (2, 0, 1)]
+    parts = [(l, t) for l in (0, 1) for t in (2, 0, 1)]
+    inward = z + 1 - 2 * h
 
     loads = []
     for t in range(3):
@@ -442,6 +481,21 @@
         for t in (2, 0, 1):
             loads[t][which].start()
 
+    near = []
+    for t in range(3):
+        block = pl.ds(pl.multiple_of((2 * inward + c) * g_s[t].shape[1], 32), g_s[t].shape[1])
+        near += [
+            pltpu.make_async_copy(lent[t], m_n[t], near_sem.at[t, 0]),
+            pltpu.make_async_copy(lent[3 + t], v_n[t], near_sem.at[t, 1]),
+            pltpu.make_async_copy(lent[6 + t], g_n[t], near_sem.at[t, 2]),
+            pltpu.make_async_copy(w_hbm[t].at[1, block], w_n[t], near_sem.at[t, 3]),
+        ]
+
+    @pl.when(end)
+    def _():
+        for copy in near:
+            copy.start()
+
     barrier = pltpu.get_barrier_semaphore()
     for other in range(1, 8):
         pl.semaphore_signal(barrier, inc=1, device_id={"dp": (me + other) % 8}, device_id_type=MESH)
@@ -515,26 +569,39 @@
             pltpu.make_async_copy(v_s[t].at[l], v_out[t].at[l], mv_sem.at[p, 1]),
         )
 
+    def adamw(g, m, v, w):
+        g, w = g.astype(F32) * factor, w.astype(F32)
+        m = 0.9 * m + 0.1 * g
+        v = 0.95 * v + 0.05 * g * g
+        return (w - 0.02 * (m * lax.rsqrt(v + 1e-8) + 0.1 * w)).astype(BF16), m, v
+
+    def sends_right(p, hop):
+        if hop == 0 and parts[p][0] == 1:
+            return jnp.logical_and(z < 3, z != 2)
+        return jnp.logical_and(z < 3, z >= hop)
+
+    def sends_left(p, hop):
+        if hop == 0 and parts[p][0] == 1:
+            return jnp.logical_and(z > 0, z != 1)
+        return jnp.logical_and(z > 0, z + hop <= 3)
+
     for p, (l, t) in enumerate(parts):
 
-        def adamw(r, _, l=l, t=t):
+        def own(r, _, l=l, t=t):
             at = strip(r)
-            g = g_s[t][l, at].astype(F32) * factor
-            w = w_s[t][l, at].astype(F32)
-            m = 0.9 * m_s[t][l, at] + 0.1 * g
-            v = 0.95 * v_s[t][l, at] + 0.05 * g * g
+            new, m, v = adamw(g_s[t][l, at], m_s[t][l, at], v_s[t][l, at], w_s[t][l, at])
             m_s[t][l, at] = m
             v_s[t][l, at] = v
-            n_s[t][l, at] = (w - 0.02 * (m * lax.rsqrt(v + 1e-8) + 0.1 * w)).astype(BF16)
+            n_s[t][l, at] = new
             return 0
 
-        lax.fori_loop(0, g_s[t].shape[1] // STEP, adamw, 0)
-
-        @pl.when(z < 3)
+        lax.fori_loop(0, g_s[t].shape[1] // STEP, own, 0)
+
+        @pl.when(sends_right(p, 0))
         def _():
             to_right(p, 0).start()
 
-        @pl.when(z > 0)
+        @pl.when(sends_left(p, 0))
         def _():
             to_left(p, 0).start()
 
@@ -543,11 +610,38 @@
         for copy in moments(p):
             copy.start()
 
+    def near_block(p):
+        return block(p, inward, c)
+
+    def near_keep(p):
+        return pltpu.make_async_copy(n_n[parts[p][1]], near_block(p), own_sem.at[p])
+
+    def near_to_partner(p):
+        return remote(n_n[parts[p][1]], near_block(p), p_send.at[p, inward], p_recv.at[p, inward], partner)
+
+    @pl.when(end)
+    def _():
+        for copy in near:
+            copy.wait()
+        for p, (l, t) in enumerate(parts):
+            if l == 1:
+
+                def neighbour(r, _, t=t):
+                    at = strip(r)
+                    n_n[t][at] = adamw(g_n[t][at], m_n[t][at], v_n[t][at], w_n[t][at])[0]
+                    return 0
+
+                lax.fori_loop(0, g_s[t].shape[1] // STEP, neighbour, 0)
+                near_to_partner(p).start()
+                keep(p).wait()
+                near_keep(p).start()
+
     n = len(parts)
     for hop in range(3):
         for p in range(n):
-
-            @pl.when(z > hop)
+            borrowed = hop == 0 and parts[p][0] == 1
+
+            @pl.when(jnp.logical_and(z > hop, z != 3) if borrowed else z > hop)
             def _():
                 to_right(p, hop).wait_recv()
 
@@ -559,7 +653,7 @@
 
                 to_partner(p, z - hop - 1).start()
 
-            @pl.when(z + hop < 3)
+            @pl.when(jnp.logical_and(z + hop < 3, z != 0) if borrowed else z + hop < 3)
             def _():
                 to_left(p, hop).wait_recv()
 
@@ -582,34 +676,36 @@
             to_partner(p, zt).wait_send()
         for hop in range(3):
 
-            @pl.when(jnp.logical_and(z < 3, z >= hop))
+            @pl.when(sends_right(p, hop))
             def _():
                 to_right(p, hop).wait_send()
 
-            @pl.when(jnp.logical_and(z > 0, z + hop <= 3))
+            @pl.when(sends_left(p, hop))
             def _():
                 to_left(p, hop).wait_send()
 
 
-def update(g, m, v, w):
+def update(g, m, v, w, lent):
     V, DMA = pltpu.VMEM, pltpu.SemaphoreType.DMA
     S = jax.ShapeDtypeStruct
     count = 8 * sum(a.size for a in g)
-    out = [S(a.shape, BF16) for a in w] + [S(a.shape, F32) for a in (*m, *v)]
+    out = [V(a.shape, BF16) for a in w] + [V(a.shape, F32) for a in (*m, *v)]
     return pl.pallas_call(
         functools.partial(update_kernel, float(count)),
         out_shape=out,
-        in_specs=[pl.BlockSpec(memory_space=pltpu.HBM)] * 12,
+        in_specs=[pl.BlockSpec(memory_space=pltpu.HBM)] * 21,
         out_specs=[pl.BlockSpec(memory_space=pl.ANY)] * 9,
         scratch_shapes=[
             *(V(a.shape, BF16) for a in g), *(V(a.shape, F32) for a in m), *(V(a.shape, F32) for a in v),
             *(V(a.shape, BF16) for a in g), *(V(a.shape, BF16) for a in g),
+            *(V(a.shape[1:], BF16) for a in g), *(V(a.shape[1:], F32) for a in m), *(V(a.shape[1:], F32) for a in v),
+            *(V(a.shape[1:], BF16) for a in g), *(V(a.shape[1:], BF16) for a in g),
             V((8, 8, 128), F32), DMA((3, 4)), DMA((8,)), DMA((8,)),
-            DMA((6, 3)), DMA((6, 3)), DMA((6, 3)), DMA((6, 3)), DMA((6, 4)), DMA((6, 4)), DMA((6,)), DMA((6, 2)),
+            DMA((6, 3)), DMA((6, 3)), DMA((6, 3)), DMA((6, 3)), DMA((6, 4)), DMA((6, 4)), DMA((6,)), DMA((6, 2)), DMA((3, 4)),
         ],
-        compiler_params=pltpu.CompilerParams(collective_id=1, has_side_effects=True, vmem_limit_bytes=18_000_000),
+        compiler_params=pltpu.CompilerParams(collective_id=1, has_side_effects=True, vmem_limit_bytes=36_000_000),
         name="update",
-    )(*g, *m, *v, *w)
+    )(*g, *m, *v, *w, *lent)
 
 
 def store_kernel(*refs):
@@ -638,8 +734,8 @@
 def solution(mesh):
     def step(x, dy, *arrays):
         w, m, v = (arrays[i : i + 3] for i in (0, 3, 6))
-        g = gradients(x[0], dy[0], *w)
-        return tuple(store(update(g, m, v, w)))
+        out = gradients(x[0], dy[0], *w, (*m, *v))
+        return tuple(store(update(out[:3], m, v, w, out[3:])))
 
     whole, split = P(None, None, None), P(None, "dp", None)
     return jax.shard_map(

time: 375 us -> 343 us (0.915)
  Pallas kernels: 362 us -> 342 us
  local copies, waits for them, and re-layouts: 11.3 us -> 0 us
    pallas_call x1, Pallas kernels: 148 us -> 123 us  [update(): pl.pallas_call(functools.partial(update_kernel, float(count)), out_shape=...]
    unnamed x18 -> x0, local copies, waits for them, and re-layouts: 11.3 us -> none
    pallas_call x1, Pallas kernels: 206 us -> 211 us  [gradients(): pl.pallas_call(functools.partial(gradients_kernel, T, D, FF), out_shape=[...]
where the time goes in v3:
time: 343 us
  Pallas kernels  342 us (100%)
    pallas_call x1, Pallas kernels, gradients(): pl.pallas_call(functools.partial(gradients_kernel, T, D, FF), out_shape=[...  211 us
    pallas_call x1, Pallas kernels, update(): pl.pallas_call(functools.partial(update_kernel, float(count)), out_shape=...  123 us
    pallas_call x1, Pallas kernels, store(): pl.pallas_call(store_kernel, out_shape=[jax.ShapeDtypeStruct(a.shape, a.d...  8.41 us

profile of v3, /device:TPU:0, one launch (start us, length us, event | category | flops | bytes accessed | tf_op | source)
XLA Modules:
  0.0 342.9 jit_solution(3089666987729713232)
XLA Ops:
  0.6 211.0 %gradients.1 = (bf16[2,96,1792]{2,1,0:T(8,128)(2,1)}, bf16[2,96,1792]{2,1,0:T(8,128)(2,1)}, bf16[2,224,768]{2,1,0:T(8,128)(2,1)}, f32[96,1792]{1,0:T(8,128)}, f3...) custom-call(bf16[2048,768]{1,0:T(8,128)(2,1)} %bitcast.2, ...), custom_call_target="tpu_custom_call" | custom-call | tf_op jit(solution)/shard_map/gradients/pallas_call | solution.py:432
  211.6 122.7 %update.1 = (bf16[2,768,1792]{2,1,0:T(8,128)(2,1)S(1)}, bf16[2,768,1792]{2,1,0:T(8,128)(2,1)S(1)}, bf16[2,1792,768]{2,1,0:T(8,128)(2,1)S(1)}, f32[2,96,1792]{2,1...) custom-call(bf16[2,96,1792]{2,1,0:T(8,128)(2,1)} %get-tuple-element., ...), custom_call_target="tpu_custom_call" | custom-call | tf_op jit(solution)/shard_map/update/pallas_call | solution.py:693
  334.4 8.4 %store.1 = (bf16[2,768,1792]{2,1,0:T(8,128)(2,1)}, bf16[2,768,1792]{2,1,0:T(8,128)(2,1)}, bf16[2,1792,768]{2,1,0:T(8,128)(2,1)}, f32[2,96,1792]{2,1,0:T(8,128)},...) custom-call(bf16[2,768,1792]{2,1,0:T(8,128)(2,1)S(1)} %get-tuple-ele, ...), custom_call_target="tpu_custom_call" | custom-call | tf_op jit(solution)/shard_map/store/pallas_call | solution.py:723

commit v4 on v3

--- a/solution.py
+++ b/solution.py
@@ -39,7 +39,7 @@
     H, A0, A1, AT, DY, ACC, hid, dg, du, wgs, wus, wds,
     own, prec, fin, RE, RM, ownd, precd, find, REd, RMd,
     w_sem, in_sem, d_send, d_recv, e_send, e_recv, m_send, m_recv,
-    dd_send, dd_recv, ed_send, ed_recv, md_send, md_recv, lend_send, lend_recv,
+    dd_send, dd_recv, ed_send, ed_recv, md_send, md_recv, lend_send, lend_recv, x_sem,
     ) = refs[18:]
     me, z, c, h, end = placed()
     partner = z * 2 + 1 - c
@@ -69,9 +69,12 @@
             pltpu.make_async_copy(wd_hbm.at[l, cols, :], wds.at[slot], w_sem.at[slot, 2]),
         )
 
-    get_x = pltpu.make_async_copy(x_hbm, H, in_sem.at[0])
-    get_dy = pltpu.make_async_copy(dy_hbm, DY, in_sem.at[1])
-    get_x.start()
+    def get_x(t):
+        return pltpu.make_async_copy(x_hbm.at[rows(t)], H.at[rows(t)], x_sem.at[t])
+
+    get_dy = pltpu.make_async_copy(dy_hbm, DY, in_sem.at[0])
+    for t in range(tiles):
+        get_x(t).start()
     for copy in weights(0, 0, 0):
         copy.start()
     get_dy.start()
@@ -91,9 +94,8 @@
     def normed(wide):
         return wide * lax.rsqrt(jnp.mean(wide * wide, -1, keepdims=True) + 1e-6)
 
-    get_x.wait()
-
     def first(t, _):
+        get_x(t).wait()
         A0[rows(t)] = normed(H[rows(t)].astype(F32)).astype(BF16)
         ACC[rows(t)] = jnp.zeros((TT, D), F32)
         return 0
@@ -174,21 +176,27 @@
     def to_end(k):
         return remote(prec.at[k, target(0)], RM.at[k, 0], m_send.at[k], m_recv.at[k, 0], outward)
 
-    def from_end_d(p, q):
-        return remote(precd.at[p, target(q)], REd.at[p, q - 1], ed_send.at[p, q - 1], ed_recv.at[p, q - 1], inward)
-
-    def across_d(p, q):
-        return remote(precd.at[p, target(q)], RMd.at[p, 3 - q], ed_send.at[p, q - 1], md_recv.at[p, 3 - q], inward)
-
-    def to_end_d(p):
-        return remote(precd.at[p, target(0)], RMd.at[p, 0], md_send.at[p], md_recv.at[p, 0], outward)
+    def half(u):
+        return pl.ds(u * (RD // 2), RD // 2)
+
+    def from_end_d(p, q, u):
+        src, dst = precd.at[p, target(q), half(u)], REd.at[p, q - 1, half(u)]
+        return remote(src, dst, ed_send.at[p, q - 1, u], ed_recv.at[p, q - 1, u], inward)
+
+    def across_d(p, q, u):
+        src, dst = precd.at[p, target(q), half(u)], RMd.at[p, 3 - q, half(u)]
+        return remote(src, dst, ed_send.at[p, q - 1, u], md_recv.at[p, 3 - q, u], inward)
+
+    def to_end_d(p, u):
+        src, dst = precd.at[p, target(0), half(u)], RMd.at[p, 0, half(u)]
+        return remote(src, dst, md_send.at[p, u], md_recv.at[p, 0, u], outward)
 
     def both(k, zt):
         return own[k % 4, zt, c].astype(F32) + prec[k, zt].astype(F32)
 
-    def both_d(p, zt):
-        block = pl.ds(pl.multiple_of((2 * zt + c) * RD, RD), RD)
-        return ownd[p, block].astype(F32) + precd[p, zt].astype(F32)
+    def both_d(p, zt, u):
+        block = pl.ds(pl.multiple_of((2 * zt + c) * RD + u * (RD // 2), RD // 2), RD // 2)
+        return ownd[p, block].astype(F32) + precd[p, zt, half(u)].astype(F32)
 
     def share(k):
         to_partner(k).wait()
@@ -206,12 +214,14 @@
 
         @pl.when(zt == z)
         def _():
-            find[p] = both_d(p, zt)
+            for u in range(2):
+                find[p, half(u)] = both_d(p, zt, u)
 
         @pl.when(jnp.logical_and(end, zt != z))
         def _():
-            precd[p, zt] = both_d(p, zt).astype(BF16)
-            from_end_d(p, q).start()
+            for u in range(2):
+                precd[p, zt, half(u)] = both_d(p, zt, u).astype(BF16)
+                from_end_d(p, q, u).start()
 
     def pass_on(k):
         @pl.when(mid)
@@ -228,19 +238,22 @@
             prec[k, target(0)] = (both(k, target(0)) + RM[k, 0].astype(F32)).astype(BF16)
             to_end(k).start()
 
-    def pass_on_d(p, q):
-        @pl.when(mid)
-        def _():
-            from_end_d(p, q).wait_recv()
-            precd[p, target(q)] = (both_d(p, target(q)) + REd[p, q - 1].astype(F32)).astype(BF16)
-            across_d(p, q).start()
+    def pass_on_d(p, q, u):
+        @pl.when(mid)
+        def _():
+            from_end_d(p, q, u).wait_recv()
+            total = both_d(p, target(q), u) + REd[p, q - 1, half(u)].astype(F32)
+            precd[p, target(q), half(u)] = total.astype(BF16)
+            across_d(p, q, u).start()
 
     def pass_back_d(p):
         @pl.when(mid)
         def _():
-            across_d(p, 3).wait_recv()
-            precd[p, target(0)] = (both_d(p, target(0)) + RMd[p, 0].astype(F32)).astype(BF16)
-            to_end_d(p).start()
+            for u in range(2):
+                across_d(p, 3, u).wait_recv()
+                total = both_d(p, target(0), u) + RMd[p, 0, half(u)].astype(F32)
+                precd[p, target(0), half(u)] = total.astype(BF16)
+                to_end_d(p, u).start()
 
     def finish(k, _):
         p, i = k // steps, k % steps
@@ -267,13 +280,15 @@
     def finish_d(p):
         @pl.when(end)
         def _():
-            to_end_d(p).wait_recv()
+            for u in range(2):
+                to_end_d(p, u).wait_recv()
             gd_ref[1 - p] = (find[p] + RMd[p, 0].astype(F32)).astype(BF16)
 
         @pl.when(mid)
         def _():
-            from_end_d(p, 1).wait_recv()
-            across_d(p, 2).wait_recv()
+            for u in range(2):
+                from_end_d(p, 1, u).wait_recv()
+                across_d(p, 2, u).wait_recv()
             gd_ref[1 - p] = (find[p] + REd[p, 0].astype(F32) + RMd[p, 1].astype(F32)).astype(BF16)
 
     def backward(p, A, i, _):
@@ -297,6 +312,9 @@
 
         lax.fori_loop(0, tiles, tile, 0)
         here = pl.ds(pl.multiple_of(j * CHUNK, CHUNK), CHUNK)
+        own[k % 4, :, :, 0] = dot(AT[...], dg[...]).astype(BF16).reshape(4, 2, RG, CHUNK)
+        own[k % 4, :, :, 1] = dot(AT[...], du[...]).astype(BF16).reshape(4, 2, RG, CHUNK)
+        to_partner(k).start()
         ownd[p, here] = dot(hid[...], DY[...], 0, 0).astype(BF16)
         zt = (i // 2 + 3) % 4
         down_ready = jnp.logical_or(i % 2 == 1, i == steps - 1)
@@ -304,10 +322,6 @@
         @pl.when(down_ready)
         def _():
             to_partner_d(p, zt).start()
-
-        own[k % 4, :, :, 0] = dot(AT[...], dg[...]).astype(BF16).reshape(4, 2, RG, CHUNK)
-        own[k % 4, :, :, 1] = dot(AT[...], du[...]).astype(BF16).reshape(4, 2, RG, CHUNK)
-        to_partner(k).start()
 
         if p == 0:
 
@@ -334,13 +348,14 @@
 
         if p == 1:
 
-            @pl.when(i == 3)
+            @pl.when(i == 2)
             def _():
-                pass_on_d(0, 3)
-                pass_on_d(0, 2)
+                for q in (3, 2):
+                    for u in range(2):
+                        pass_on_d(0, q, u)
                 pass_back_d(0)
 
-            @pl.when(jnp.logical_and(mid, i == 5))
+            @pl.when(jnp.logical_and(mid, i == 3))
             def _():
                 finish_d(0)
                 lax.fori_loop(0, steps, finish, 0)
@@ -365,10 +380,12 @@
     lax.fori_loop(0, steps, functools.partial(backward, 1, A0), 0)
 
     last = 2 * steps - 1
-    pass_on_d(1, 3)
+    pass_on_d(1, 3, 0)
+    pass_on_d(1, 3, 1)
     pass_on(last - 1)
-    pass_on_d(1, 2)
+    pass_on_d(1, 2, 0)
     pass_on(last)
+    pass_on_d(1, 2, 1)
     pass_back_d(1)
     pass_back(last - 2)
     pass_back(last - 1)
@@ -412,14 +429,16 @@
 
         @pl.when(end)
         def _():
-            for q in (3, 2, 1):
-                from_end_d(p, q).wait_send()
-
-        @pl.when(mid)
-        def _():
-            across_d(p, 3).wait_send()
-            across_d(p, 2).wait_send()
-            to_end_d(p).wait_send()
+            for u in range(2):
+                for q in (3, 2, 1):
+                    from_end_d(p, q, u).wait_send()
+
+        @pl.when(mid)
+        def _():
+            for u in range(2):
+                across_d(p, 3, u).wait_send()
+                across_d(p, 2, u).wait_send()
+                to_end_d(p, u).wait_send()
 
 
 def gradients(x, dy, wg, wu, wd, moments):
@@ -432,9 +451,9 @@
     return pl.pallas_call(
         functools.partial(gradients_kernel, T, D, FF),
         out_shape=[
-            jax.ShapeDtypeStruct((L, RG, FF), BF16),
-            jax.ShapeDtypeStruct((L, RG, FF), BF16),
-            jax.ShapeDtypeStruct((L, RD, D), BF16),
+            V((L, RG, FF), BF16),
+            V((L, RG, FF), BF16),
+            V((L, RD, D), BF16),
             *(pltpu.HBM(a.shape[1:], F32) for a in moments),
             *(pltpu.HBM(a.shape[1:], BF16) for a in moments[:3]),
         ],
@@ -448,19 +467,19 @@
             V((n, 3, *piece), BF16), V((n, 2, *piece), BF16),
             V((L, FF, D), BF16), V((L, 4, RD, D), BF16), V((L, RD, D), F32),
             V((L, 3, RD, D), BF16), V((L, 2, RD, D), BF16),
-            DMA((2, 3)), DMA((2,)), DMA((n,)), DMA((n,)), DMA((n, 3)), DMA((n, 3)), DMA((n,)), DMA((n, 2)),
-            DMA((L, 4)), DMA((L, 4)), DMA((L, 3)), DMA((L, 3)), DMA((L,)), DMA((L, 2)), DMA((9,)), DMA((9,)),
+            DMA((2, 3)), DMA((1,)), DMA((n,)), DMA((n,)), DMA((n, 3)), DMA((n, 3)), DMA((n,)), DMA((n, 2)),
+            DMA((L, 4)), DMA((L, 4)), DMA((L, 3, 2)), DMA((L, 3, 2)), DMA((L, 2)), DMA((L, 2, 2)), DMA((9,)), DMA((9,)), DMA((T // min(512, T),)),
         ],
-        compiler_params=pltpu.CompilerParams(collective_id=0, has_side_effects=True, vmem_limit_bytes=VMEM_LIMIT),
+        compiler_params=pltpu.CompilerParams(collective_id=0, has_side_effects=True, vmem_limit_bytes=VMEM_LIMIT - 5_000_000),
         name="gradients",
     )(x, dy, wg, wu, wd, *moments)
 
 
 def update_kernel(count, *refs):
-    g_hbm, m_hbm, v_hbm, w_hbm, lent = refs[0:3], refs[3:6], refs[6:9], refs[9:12], refs[12:21]
+    g_s, m_hbm, v_hbm, w_hbm, lent = refs[0:3], refs[3:6], refs[6:9], refs[9:12], refs[12:21]
     w_out, m_out, v_out, refs = refs[21:24], refs[24:27], refs[27:30], refs[30:]
-    g_s, m_s, v_s, w_s, n_s = refs[0:3], refs[3:6], refs[6:9], refs[9:12], refs[12:15]
-    g_n, m_n, v_n, w_n, n_n, refs = refs[15:18], refs[18:21], refs[21:24], refs[24:27], refs[27:30], refs[30:]
+    m_s, v_s, w_s, n_s, refs = refs[0:3], refs[3:6], refs[6:9], refs[9:12], refs[12:]
+    g_n, m_n, v_n, w_n, n_n, refs = refs[0:3], refs[3:6], refs[6:9], refs[9:12], refs[12:15], refs[15:]
     sq, in_sem, sq_send, sq_recv, r_send, r_recv, l_send, l_recv, p_send, p_recv, own_sem, mv_sem, near_sem = refs
     me, z, c, h, end = placed()
     partner = z * 2 + 1 - c
@@ -472,12 +491,11 @@
     for t in range(3):
         block = pl.ds(pl.multiple_of(me * g_s[t].shape[1], 32), g_s[t].shape[1])
         loads.append([
-            pltpu.make_async_copy(g_hbm[t], g_s[t], in_sem.at[t, 0]),
-            pltpu.make_async_copy(m_hbm[t], m_s[t], in_sem.at[t, 1]),
-            pltpu.make_async_copy(v_hbm[t], v_s[t], in_sem.at[t, 2]),
-            pltpu.make_async_copy(w_hbm[t].at[:, block], w_s[t], in_sem.at[t, 3]),
+            pltpu.make_async_copy(m_hbm[t], m_s[t], in_sem.at[t, 0]),
+            pltpu.make_async_copy(v_hbm[t], v_s[t], in_sem.at[t, 1]),
+            pltpu.make_async_copy(w_hbm[t].at[:, block], w_s[t], in_sem.at[t, 2]),
         ])
-    for which in range(4):
+    for which in range(3):
         for t in (2, 0, 1):
             loads[t][which].start()
 
@@ -507,7 +525,6 @@
 
     total = jnp.zeros((8, 128), F32)
     for t in range(3):
-        loads[t][0].wait()
         R, C = g_s[t].shape[1:]
 
         def squares(r, total, t=t, R=R, C=C):
@@ -530,7 +547,7 @@
     for other in range(1, 8):
         tell(other).start()
     for t in range(3):
-        for which in (1, 2, 3):
+        for which in range(3):
             loads[t][which].wait()
     for other in range(1, 8):
         told(other).wait_recv()
@@ -693,19 +710,19 @@
     return pl.pallas_call(
         functools.partial(update_kernel, float(count)),
         out_shape=out,
-        in_specs=[pl.BlockSpec(memory_space=pltpu.HBM)] * 21,
+        in_specs=[pl.BlockSpec(memory_space=pltpu.VMEM)] * 3 + [pl.BlockSpec(memory_space=pltpu.HBM)] * 18,
         out_specs=[pl.BlockSpec(memory_space=pl.ANY)] * 9,
         scratch_shapes=[
-            *(V(a.shape, BF16) for a in g), *(V(a.shape, F32) for a in m), *(V(a.shape, F32) for a in v),
+            *(V(a.shape, F32) for a in m), *(V(a.shape, F32) for a in v),
             *(V(a.shape, BF16) for a in g), *(V(a.shape, BF16) for a in g),
             *(V(a.shape[1:], BF16) for a in g), *(V(a.shape[1:], F32) for a in m), *(V(a.shape[1:], F32) for a in v),
             *(V(a.shape[1:], BF16) for a in g), *(V(a.shape[1:], BF16) for a in g),
-            V((8, 8, 128), F32), DMA((3, 4)), DMA((8,)), DMA((8,)),
+            V((8, 8, 128), F32), DMA((3, 3)), DMA((8,)), DMA((8,)),
             DMA((6, 3)), DMA((6, 3)), DMA((6, 3)), DMA((6, 3)), DMA((6, 4)), DMA((6, 4)), DMA((6,)), DMA((6, 2)), DMA((3, 4)),
         ],
         compiler_params=pltpu.CompilerParams(collective_id=1, has_side_effects=True, vmem_limit_bytes=36_000_000),
         name="update",
-    )(*g, *m, *v, *w, *lent)
+    )(*(pltpu.with_memory_space_constraint(a, pltpu.VMEM) for a in g), *m, *v, *w, *lent)
 
 
 def store_kernel(*refs):

time: 343 us -> 335 us (0.977)
  Pallas kernels: 342 us -> 334 us
    pallas_call x1, Pallas kernels: 211 us -> 200 us  [gradients(): pl.pallas_call(functools.partial(gradients_kernel, T, D, FF), out_shape=[...]
where the time goes in v4:
time: 335 us
  Pallas kernels  334 us (100%)
    pallas_call x1, Pallas kernels, gradients(): pl.pallas_call(functools.partial(gradients_kernel, T, D, FF), out_shape=[...  200 us
    pallas_call x1, Pallas kernels, update(): pl.pallas_call(functools.partial(update_kernel, float(count)), out_shape=...  126 us
    pallas_call x1, Pallas kernels, store(): pl.pallas_call(store_kernel, out_shape=[jax.ShapeDtypeStruct(a.shape, a.d...  8.41 us

profile of v4, /device:TPU:0, one launch (start us, length us, event | category | flops | bytes accessed | tf_op | source)
XLA Modules:
  0.0 334.9 jit_solution(7184204855263910017)
XLA Ops:
  0.6 199.5 %gradients.1 = (bf16[2,96,1792]{2,1,0:T(8,128)(2,1)S(1)}, bf16[2,96,1792]{2,1,0:T(8,128)(2,1)S(1)}, bf16[2,224,768]{2,1,0:T(8,128)(2,1)S(1)}, f32[96,1792]{1,0:T...) custom-call(bf16[2048,768]{1,0:T(8,128)(2,1)} %bitcast.2, ...), custom_call_target="tpu_custom_call" | custom-call | tf_op jit(solution)/shard_map/gradients/pallas_call | solution.py:451
  200.2 126.1 %update.1 = (bf16[2,768,1792]{2,1,0:T(8,128)(2,1)S(1)}, bf16[2,768,1792]{2,1,0:T(8,128)(2,1)S(1)}, bf16[2,1792,768]{2,1,0:T(8,128)(2,1)S(1)}, f32[2,96,1792]{2,1...) custom-call(bf16[2,96,1792]{2,1,0:T(8,128)(2,1)S(1)} %get-tuple-elem, ...), custom_call_target="tpu_custom_call" | custom-call | tf_op jit(solution)/shard_map/update/pallas_call | solution.py:710
  326.3 8.4 %store.1 = (bf16[2,768,1792]{2,1,0:T(8,128)(2,1)}, bf16[2,768,1792]{2,1,0:T(8,128)(2,1)}, bf16[2,1792,768]{2,1,0:T(8,128)(2,1)}, f32[2,96,1792]{2,1,0:T(8,128)},...) custom-call(bf16[2,768,1792]{2,1,0:T(8,128)(2,1)S(1)} %get-tuple-ele, ...), custom_call_target="tpu_custom_call" | custom-call | tf_op jit(solution)/shard_map/store/pallas_call | solution.py:740

commit v5 on v4

--- a/solution.py
+++ b/solution.py
@@ -60,6 +60,11 @@
     def rows(t):
         return pl.ds(pl.multiple_of(t * TT, TT), TT)
 
+    TB = min(1024, T)
+
+    def big(t):
+        return pl.ds(pl.multiple_of(t * TB, TB), TB)
+
     def weights(l, i, s):
         cols = pl.ds(pl.multiple_of(column(i) * CHUNK, CHUNK), CHUNK)
         slot = s % 2
@@ -134,15 +139,15 @@
         slot = i % 2
 
         def tile(t, _):
-            a = A0[rows(t)]
+            a = A0[big(t)]
             gate, up = dot(a, wgs[slot]), dot(a, wus[slot])
             hidden = (gate * lax.logistic(gate) * up).astype(BF16)
             down = dot(hidden, wds[slot])
 
-            ACC[rows(t)] += down
+            ACC[big(t)] += down
             return 0
 
-        lax.fori_loop(0, tiles, tile, 0)
+        lax.fori_loop(0, T // TB, tile, 0)
         return 0
 
     lax.fori_loop(0, steps, forward, 0)
@@ -300,17 +305,17 @@
         next_weights(l, i, s, 0 if p == 0 else None)
 
         def tile(t, _):
-            a = A[rows(t)]
+            a = A[big(t)]
             gate, up = dot(a, wgs[slot]), dot(a, wus[slot])
-            dh = dot(DY[rows(t)], wds[slot], 1, 1).astype(BF16).astype(F32)
+            dh = dot(DY[big(t)], wds[slot], 1, 1).astype(BF16).astype(F32)
             sig = lax.logistic(gate)
             act = gate * sig
-            hid[rows(t)] = (act * up).astype(BF16)
-            du[rows(t)] = (dh * act).astype(BF16)
-            dg[rows(t)] = (dh * up * (sig * (1.0 + gate * (1.0 - sig)))).astype(BF16)
+            hid[big(t)] = (act * up).astype(BF16)
+            du[big(t)] = (dh * act).astype(BF16)
+            dg[big(t)] = (dh * up * (sig * (1.0 + gate * (1.0 - sig)))).astype(BF16)
             return 0
 
-        lax.fori_loop(0, tiles, tile, 0)
+        lax.fori_loop(0, T // TB, tile, 0)
         here = pl.ds(pl.multiple_of(j * CHUNK, CHUNK), CHUNK)
         own[k % 4, :, :, 0] = dot(AT[...], dg[...]).astype(BF16).reshape(4, 2, RG, CHUNK)
         own[k % 4, :, :, 1] = dot(AT[...], du[...]).astype(BF16).reshape(4, 2, RG, CHUNK)
@@ -325,18 +330,24 @@
 
         if p == 0:
 
+            @pl.when(i == 0)
+            def _():
+                share(k)
+
             def back(t, _):
-                da = dot(dg[rows(t)], wgs[slot], 1, 1) + dot(du[rows(t)], wus[slot], 1, 1)
-                ACC[rows(t)] += da
+                da = dot(dg[big(t)], wgs[slot], 1, 1) + dot(du[big(t)], wus[slot], 1, 1)
+                ACC[big(t)] += da
                 return 0
 
-            lax.fori_loop(0, tiles, back, 0)
+            lax.fori_loop(0, T // TB, back, 0)
 
         @pl.when(down_ready)
         def _():
             share_d(p, zt)
 
-        share(k)
+        @pl.when(k > 0)
+        def _():
+            share(k)
 
         @pl.when(k >= 2)
         def _():
@@ -470,7 +481,7 @@
             DMA((2, 3)), DMA((1,)), DMA((n,)), DMA((n,)), DMA((n, 3)), DMA((n, 3)), DMA((n,)), DMA((n, 2)),
             DMA((L, 4)), DMA((L, 4)), DMA((L, 3, 2)), DMA((L, 3, 2)), DMA((L, 2)), DMA((L, 2, 2)), DMA((9,)), DMA((9,)), DMA((T // min(512, T),)),
         ],
-        compiler_params=pltpu.CompilerParams(collective_id=0, has_side_effects=True, vmem_limit_bytes=VMEM_LIMIT - 5_000_000),
+        compiler_params=pltpu.CompilerParams(collective_id=0, has_side_effects=True, vmem_limit_bytes=VMEM_LIMIT - 2_300_000),
         name="gradients",
     )(x, dy, wg, wu, wd, *moments)
 

time: 335 us -> 327 us (0.976)
  Pallas kernels: 334 us -> 326 us
    pallas_call x1, Pallas kernels: 200 us -> 191 us  [gradients(): pl.pallas_call(functools.partial(gradients_kernel, T, D, FF), out_shape=[...]
where the time goes in v5:
time: 327 us
  Pallas kernels  326 us (100%)
    pallas_call x1, Pallas kernels, gradients(): pl.pallas_call(functools.partial(gradients_kernel, T, D, FF), out_shape=[...  191 us
    pallas_call x1, Pallas kernels, update(): pl.pallas_call(functools.partial(update_kernel, float(count)), out_shape=...  127 us
    pallas_call x1, Pallas kernels, store(): pl.pallas_call(store_kernel, out_shape=[jax.ShapeDtypeStruct(a.shape, a.d...  8.41 us

profile of v5, /device:TPU:0, one launch (start us, length us, event | category | flops | bytes accessed | tf_op | source)
XLA Modules:
  0.0 326.8 jit_solution(10839864037563324973)
XLA Ops:
  0.6 190.6 %gradients.1 = (bf16[2,96,1792]{2,1,0:T(8,128)(2,1)S(1)}, bf16[2,96,1792]{2,1,0:T(8,128)(2,1)S(1)}, bf16[2,224,768]{2,1,0:T(8,128)(2,1)S(1)}, f32[96,1792]{1,0:T...) custom-call(bf16[2048,768]{1,0:T(8,128)(2,1)} %bitcast.2, ...), custom_call_target="tpu_custom_call" | custom-call | tf_op jit(solution)/shard_map/gradients/pallas_call | solution.py:462
  191.3 127.0 %update.1 = (bf16[2,768,1792]{2,1,0:T(8,128)(2,1)S(1)}, bf16[2,768,1792]{2,1,0:T(8,128)(2,1)S(1)}, bf16[2,1792,768]{2,1,0:T(8,128)(2,1)S(1)}, f32[2,96,1792]{2,1...) custom-call(bf16[2,96,1792]{2,1,0:T(8,128)(2,1)S(1)} %get-tuple-elem, ...), custom_call_target="tpu_custom_call" | custom-call | tf_op jit(solution)/shard_map/update/pallas_call | solution.py:721
  318.3 8.4 %store.1 = (bf16[2,768,1792]{2,1,0:T(8,128)(2,1)}, bf16[2,768,1792]{2,1,0:T(8,128)(2,1)}, bf16[2,1792,768]{2,1,0:T(8,128)(2,1)}, f32[2,96,1792]{2,1,0:T(8,128)},...) custom-call(bf16[2,768,1792]{2,1,0:T(8,128)(2,1)S(1)} %get-tuple-ele, ...), custom_call_target="tpu_custom_call" | custom-call | tf_op jit(solution)/shard_map/store/pallas_call | solution.py:751

commit v6 on v5

--- a/solution.py
+++ b/solution.py
@@ -173,7 +173,13 @@
         return remote(ownd.at[p, block], precd.at[p, zt], dd_send.at[p, zt], dd_recv.at[p, zt], partner)
 
     def from_end(k, q):
-        return remote(prec.at[k, target(q)], RE.at[k, q - 1], e_send.at[k, q - 1], e_recv.at[k, q - 1], inward)
+        return remote(prec.at[k, target(q)], RE.at[k, slot_of(q)], e_send.at[k, q - 1], e_recv.at[k, q - 1], inward)
+
+    def slot_of(q):
+        return target(q) - (1 - h)
+
+    def all_from_end(k):
+        return remote(prec.at[k, pl.ds(1 - h, 3)], RE.at[k], e_send.at[k, 0], e_recv.at[k, 0], inward)
 
     def across(k, q):
         return remote(prec.at[k, target(q)], RM.at[k, 3 - q], e_send.at[k, q - 1], m_recv.at[k, 3 - q], inward)
@@ -211,7 +217,15 @@
         def _():
             for q in (3, 2, 1):
                 prec[k, target(q)] = both(k, target(q)).astype(BF16)
-                from_end(k, q).start()
+
+            @pl.when(k < 2 * steps - 1)
+            def _():
+                all_from_end(k).start()
+
+            @pl.when(k == 2 * steps - 1)
+            def _():
+                for q in (3, 2, 1):
+                    from_end(k, q).start()
 
     def share_d(p, zt):
         to_partner_d(p, zt).wait()
@@ -228,12 +242,15 @@
                 precd[p, zt, half(u)] = both_d(p, zt, u).astype(BF16)
                 from_end_d(p, q, u).start()
 
-    def pass_on(k):
+    def pass_on(k, apart=False):
         @pl.when(mid)
         def _():
+            if not apart:
+                all_from_end(k).wait_recv()
             for q in (3, 2):
-                from_end(k, q).wait_recv()
-                prec[k, target(q)] = (both(k, target(q)) + RE[k, q - 1].astype(F32)).astype(BF16)
+                if apart:
+                    from_end(k, q).wait_recv()
+                prec[k, target(q)] = (both(k, target(q)) + RE[k, slot_of(q)].astype(F32)).astype(BF16)
                 across(k, q).start()
 
     def pass_back(k):
@@ -276,9 +293,12 @@
 
         @pl.when(mid)
         def _():
-            from_end(k, 1).wait_recv()
+            @pl.when(k == 2 * steps - 1)
+            def _():
+                from_end(k, 1).wait_recv()
+
             across(k, 2).wait_recv()
-            put(fin[k] + RE[k, 0].astype(F32) + RM[k, 1].astype(F32))
+            put(fin[k] + RE[k, slot_of(1)].astype(F32) + RM[k, 1].astype(F32))
 
         return 0
 
@@ -395,7 +415,7 @@
     pass_on_d(1, 3, 1)
     pass_on(last - 1)
     pass_on_d(1, 2, 0)
-    pass_on(last)
+    pass_on(last, True)
     pass_on_d(1, 2, 1)
     pass_back_d(1)
     pass_back(last - 2)
@@ -424,8 +444,14 @@
     def sent(k, _):
         @pl.when(end)
         def _():
-            for q in (3, 2, 1):
-                from_end(k, q).wait_send()
+            @pl.when(k < last)
+            def _():
+                all_from_end(k).wait_send()
+
+            @pl.when(k == last)
+            def _():
+                for q in (3, 2, 1):
+                    from_end(k, q).wait_send()
 
         @pl.when(mid)
         def _():
@@ -529,7 +555,7 @@
     for other in range(1, 8):
         pl.semaphore_signal(barrier, inc=1, device_id={"dp": (me + other) % 8}, device_id_type=MESH)
 
-    STEP = 16
+    STEP = 32
 
     def strip(r):
         return pl.ds(pl.multiple_of(r * STEP, STEP), STEP)

time: 327 us -> 328 us (level)
  no operation moved by 1% of the time
where the time goes in v6:
time: 328 us
  Pallas kernels  327 us (100%)
    pallas_call x1, Pallas kernels, gradients(): pl.pallas_call(functools.partial(gradients_kernel, T, D, FF), out_shape=[...  193 us
    pallas_call x1, Pallas kernels, update(): pl.pallas_call(functools.partial(update_kernel, float(count)), out_shape=...  126 us
    pallas_call x1, Pallas kernels, store(): pl.pallas_call(store_kernel, out_shape=[jax.ShapeDtypeStruct(a.shape, a.d...  8.41 us

profile of v6, /device:TPU:0, one launch (start us, length us, event | category | flops | bytes accessed | tf_op | source)
XLA Modules:
  0.0 328.1 jit_solution(5196194265437627467)
XLA Ops:
  0.6 192.9 %gradients.1 = (bf16[2,96,1792]{2,1,0:T(8,128)(2,1)S(1)}, bf16[2,96,1792]{2,1,0:T(8,128)(2,1)S(1)}, bf16[2,224,768]{2,1,0:T(8,128)(2,1)S(1)}, f32[96,1792]{1,0:T...) custom-call(bf16[2048,768]{1,0:T(8,128)(2,1)} %bitcast.2, ...), custom_call_target="tpu_custom_call" | custom-call | tf_op jit(solution)/shard_map/gradients/pallas_call | solution.py:488
  193.6 126.0 %update.1 = (bf16[2,768,1792]{2,1,0:T(8,128)(2,1)S(1)}, bf16[2,768,1792]{2,1,0:T(8,128)(2,1)S(1)}, bf16[2,1792,768]{2,1,0:T(8,128)(2,1)S(1)}, f32[2,96,1792]{2,1...) custom-call(bf16[2,96,1792]{2,1,0:T(8,128)(2,1)S(1)} %get-tuple-elem, ...), custom_call_target="tpu_custom_call" | custom-call | tf_op jit(solution)/shard_map/update/pallas_call | solution.py:747
  319.6 8.4 %store.1 = (bf16[2,768,1792]{2,1,0:T(8,128)(2,1)}, bf16[2,768,1792]{2,1,0:T(8,128)(2,1)}, bf16[2,1792,768]{2,1,0:T(8,128)(2,1)}, f32[2,96,1792]{2,1,0:T(8,128)},...) custom-call(bf16[2,768,1792]{2,1,0:T(8,128)(2,1)S(1)} %get-tuple-ele, ...), custom_call_target="tpu_custom_call" | custom-call | tf_op jit(solution)/shard_map/store/pallas_call | solution.py:777
